TPU v7x, 256 devices: a whole 4x4x8 slice. The times are simulated.
256 devices in a mesh: dp: 64 (over z, y, core), mp: 4 (over x).
Axes of the slice: x: 4, y: 4, z: 8, core: 2. Of those that a mesh axis runs over, the one named last changes fastest.
Arguments:
- sample_inputs: bfloat16 [512, 512], P(('dp', 'mp')), may hold values from -6 to 6
- sample_outputs: bfloat16 [512, 1024], P(('dp', 'mp')), may hold values from -6 to 6
- directions: bfloat16 [512, 256, 512], P(('dp', 'mp')), may hold values from -24 to 24
- jacobian_targets: bfloat16 [512, 256, 1024], P(('dp', 'mp')), may hold values from -24 to 24
- jacobian_ranks: int32 [512], P(('dp', 'mp')), may hold values from 16 to 256, as said below
- encoder_weight: bfloat16 [512, 2048], replicated, may hold values from -0.25 to 0.25
- decoder_weight: bfloat16 [1024, 2048], replicated, may hold values from -0.125 to 0.125
Outputs:
- grad_encoder: float32 [512, 2048], P('dp', 'mp')
- grad_decoder: float32 [1024, 2048], P('dp', 'mp')
Inputs may be any that keep to these rules, and one draw needn't show every extreme that they name: `jacobian_ranks`: every rank is a multiple of 16.
All inputs are finite; a program needn't handle non-finite values.
Results may differ from a plain program's by a relative error of at most 0.0013.
Values may be sent and summed in bfloat16 or wider, within the bound.
No kernel may reach another device: no remote copies, remote signals or barrier semaphores. Data moves between devices by JAX's collectives and lax.ppermute only.
A program may use at most 128 MiB of HBM per device.

v0:
```python
import math

import jax
import jax.numpy as jnp
from jax import lax
from jax.sharding import PartitionSpec as P

BLK = 16


contract_last = (((1,), (1,)), ((), ()))
contract_first = (((0,), (0,)), ((), ()))
tile_blocks = 64


def cut_along(value, dim, devices):
    before, after = (value.shape[:dim], value.shape[dim + 1 :])
    return jnp.moveaxis(value.reshape(*before, devices, -1, *after), dim, 0)


def sum_together(arrays, axis, dims):
    devices = lax.axis_size(axis)
    pieces = [cut_along(a, dim, devices) for a, dim in zip(arrays, dims)]
    lines = jnp.concatenate([b.reshape(devices, -1) for b in pieces], axis=1)
    width = max(16, -(-lines.shape[1] // 1024) * 8)
    lines = jnp.pad(lines, ((0, 0), (0, width * 128 - lines.shape[1]))).reshape(-1, 128)
    ravelled, at, gathered = (lax.psum_scatter(lines, axis, tiled=True).reshape(-1), 0, [])
    for b in pieces:
        part = b[0]
        gathered.append(ravelled[at : at + part.size].reshape(part.shape))
        at += part.size
    return tuple(gathered)


def sent_and_summed(value, axis, dim):
    pieces = cut_along(value, dim, lax.axis_size(axis))
    arrived = lax.all_to_all(pieces, axis, split_axis=0, concat_axis=0, tiled=True)
    return arrived.sum(axis=0)


def side_by_side(arrays, axis, dim, along):
    ends, at = ([], 0)
    for a in arrays[:-1]:
        at += a.shape[along]
        ends.append(at)
    both = jnp.concatenate(arrays, axis=along)
    return tuple(jnp.split(sent_and_summed(both, axis, dim), ends, axis=along))


def misfit_terms(sample_inputs, sample_outputs, encoder_weight, decoder_weight, factor):
    pre_act = jnp.dot(sample_inputs, encoder_weight, preferred_element_type=jnp.float32)
    hidden_act = jnp.tanh(pre_act)
    slopes = 1.0 - hidden_act * hidden_act
    act_rounded = hidden_act.astype(jnp.bfloat16)
    fitted = lax.dot_general(
        act_rounded, decoder_weight, contract_last, preferred_element_type=jnp.float32
    )
    misfit = fitted - sample_outputs.astype(jnp.float32)
    misfit_grad = (factor * misfit).astype(jnp.bfloat16)
    grad_decoder = lax.dot_general(
        misfit_grad, act_rounded, contract_first, preferred_element_type=jnp.float32
    )
    back_misfit = jnp.dot(misfit_grad, decoder_weight, preferred_element_type=jnp.float32)
    entered = (back_misfit * slopes).astype(jnp.bfloat16)
    grad_encoder = lax.dot_general(
        sample_inputs, entered, contract_first, preferred_element_type=jnp.float32
    )
    return (grad_encoder, grad_decoder)


def block_terms(
    block_dirs, block_targets, row_values, weights, encoder_weight, decoder_weight, totals
):
    grad_encoder, grad_decoder = totals
    count_blocks = block_dirs.shape[0]
    block_cols = block_dirs.shape[1]
    in_width = block_dirs.shape[2]
    out_width = block_targets.shape[2]
    hidden = encoder_weight.shape[1]
    pre_act = jnp.dot(row_values, encoder_weight, preferred_element_type=jnp.float32)
    hidden_act = jnp.tanh(pre_act)
    slopes = 1.0 - hidden_act * hidden_act
    columns = block_dirs.reshape(count_blocks * block_cols, in_width)
    along_hidden = jnp.dot(columns, encoder_weight, preferred_element_type=jnp.float32)
    along_hidden = along_hidden.reshape(count_blocks, block_cols, hidden)
    pushed = (
        (along_hidden * slopes[:, None, :])
        .astype(jnp.bfloat16)
        .reshape(count_blocks * block_cols, hidden)
    )
    images = lax.dot_general(
        pushed, decoder_weight, contract_last, preferred_element_type=jnp.float32
    )
    misfit_cols = images.reshape(count_blocks, block_cols, out_width) - block_targets.astype(
        jnp.float32
    )
    jac_grad = (
        (misfit_cols * weights[:, None, None])
        .astype(jnp.bfloat16)
        .reshape(count_blocks * block_cols, out_width)
    )
    grad_decoder = grad_decoder + lax.dot_general(
        jac_grad, pushed, contract_first, preferred_element_type=jnp.float32
    )
    backward = jnp.dot(jac_grad, decoder_weight, preferred_element_type=jnp.float32).reshape(
        count_blocks, block_cols, hidden
    )
    lifted = (
        (backward * slopes[:, None, :])
        .astype(jnp.bfloat16)
        .reshape(count_blocks * block_cols, hidden)
    )
    curvature = -2.0 * hidden_act[:, None, :] * slopes[:, None, :] * backward * along_hidden
    sum_curve = jnp.sum(curvature, axis=1)
    grad_encoder = grad_encoder + lax.dot_general(
        columns, lifted, contract_first, preferred_element_type=jnp.float32
    )
    grad_encoder = grad_encoder + lax.dot_general(
        row_values.astype(jnp.float32), sum_curve, contract_first, precision=lax.Precision.HIGHEST
    )
    return (grad_encoder, grad_decoder)


def per_device(
    sample_inputs,
    sample_outputs,
    directions,
    jacobian_targets,
    jacobian_ranks,
    encoder_weight,
    decoder_weight,
):
    samples_here = sample_inputs.shape[0]
    in_width = sample_inputs.shape[1]
    out_width = sample_outputs.shape[1]
    per_sample = directions.shape[1] // BLK
    slot_total = samples_here * per_sample
    population = samples_here * lax.axis_size("dp") * lax.axis_size("mp")
    factor = 2.0 / math.sqrt(population)
    totals = misfit_terms(sample_inputs, sample_outputs, encoder_weight, decoder_weight, factor)
    flat_dirs = directions.reshape(slot_total, BLK, in_width)
    flat_targets = jacobian_targets.reshape(slot_total, BLK, out_width)
    counts = jacobian_ranks // BLK
    positions = jnp.arange(slot_total, dtype=jnp.int32)
    owners_all = positions // per_sample
    active = positions % per_sample < counts[owners_all]
    ordering = jnp.argsort(jnp.where(active, positions, positions + slot_total))
    held_count = jnp.sum(active.astype(jnp.int32))
    slot_weight = factor * (1.0 / jnp.maximum(counts[owners_all], 1).astype(jnp.float32))
    padded_order = jnp.concatenate([ordering, jnp.zeros((tile_blocks,), jnp.int32)])

    def tile_step(step_index, state):
        first_slot = step_index * tile_blocks
        chosen_slots = lax.dynamic_slice(padded_order, (first_slot,), (tile_blocks,))
        in_use = first_slot + jnp.arange(tile_blocks, dtype=jnp.int32) < held_count
        weights = jnp.where(in_use, slot_weight[chosen_slots], 0.0)
        row_values = jnp.take(sample_inputs, owners_all[chosen_slots], axis=0)
        return block_terms(
            jnp.take(flat_dirs, chosen_slots, axis=0),
            jnp.take(flat_targets, chosen_slots, axis=0),
            row_values,
            weights,
            encoder_weight,
            decoder_weight,
            state,
        )

    trips = (held_count + tile_blocks - 1) // tile_blocks
    grad_encoder, grad_decoder = lax.fori_loop(0, trips, tile_step, totals)
    grad_encoder, grad_decoder = sum_together((grad_encoder, grad_decoder), "dp", (0, 0))
    grad_encoder, grad_decoder = side_by_side((grad_encoder, grad_decoder), "mp", 1, 0)
    return (grad_encoder, grad_decoder)


def solution(mesh):
    in_specs = (
        P(("dp", "mp"), None),
        P(("dp", "mp"), None),
        P(("dp", "mp"), None, None),
        P(("dp", "mp"), None, None),
        P(("dp", "mp")),
        P(),
        P(),
    )
    out_specs = (P("dp", "mp"), P("dp", "mp"))
    return jax.shard_map(
        per_device, mesh=mesh, in_specs=in_specs, out_specs=out_specs, check_vma=False
    )
```

profile of v0, /device:TPU:8, one launch (start us, length us, event | category | flops | bytes accessed | tf_op | source)
XLA Modules:
  0.0 319.8 jit_solution(11356239776495338105)
XLA Ops:
  7.2 0.0 copy-start
  7.2 0.0 reduce-scatter.2.cloned.1.call-start
  7.2 0.7 and_select_fusion.3
  7.9 0.6 fusion.39
  8.5 1.9 add_select_fusion
  11.0 2.0 convolution_tanh_fusion.1
  13.0 3.4 %fusion.29 = bf16[2,1024]{1,0:T(2,128)(2,1)S(1)} fusion(bf16[1024,2048]{1,0:T(8,128)(2,1)} %param.15, bf16[2,1024]{1,0:T(2,128)(2,1)} %param.10, f32[2,2048]{1,0:T(2,128)S(1)} %convolution_tanh_fusion.1), kind=kOutput, calls=%fused_computation.66 | convolution fusion | flops 8400896 | bytes 4218880 | tf_op jit(solution)/shard_map/dot_general | solution.py:55
  16.4 0.0 copy-done
  16.4 5.3 %convolution_bitcast_fusion = f32[512,2048]{0,1:T(8,128)} fusion(bf16[2,512]{1,0:T(2,128)(2,1)S(1)} %copy-done, bf16[2,1024]{1,0:T(2,128)(2,1)S(1)} %fusion.29, bf16[1024,2048]{1,0:T(8,128)(2,1)} %param.15, f32[2,2048]{1,0:T(2,128)S(1)} %convolution_tanh_fusion.1), kind=kOutput, calls=%fused_computation.60 | convolution fusion | flops 12599296 | bytes 8411136 | tf_op jit(solution)/shard_map/dot_general | solution.py:65
  21.8 4.5 %fusion.33 = f32[1024,2048]{1,0:T(8,128)} fusion(bf16[2,1024]{1,0:T(2,128)(2,1)S(1)} %fusion.29, f32[2,2048]{1,0:T(2,128)S(1)} %convolution_tanh_fusion.1), kind=kOutput, calls=%fused_computation.71 | convolution fusion | flops 8392704 | bytes 8409088 | tf_op jit(solution)/shard_map/dot_general | solution.py:60
  26.3 1.7 sort.17
  28.0 5.6 %copy.20 = f32[512,2048]{1,0:T(8,128)} copy(f32[512,2048]{0,1:T(8,128)} %convolution_bitcast_fusion) | data formatting | bytes 8388608
  33.5 0.0 copy-done.4
  33.6 0.0 copy-done.6
  33.6 66.1 %while.13 = (s32[]{:T(128)}, f32[512,2048]{1,0:T(8,128)}, f32[1024,2048]{1,0:T(8,128)}, s32[]{:T(128)}, s32[96]{0:T(128)S(1)}, /*index=5*/bf16[32,16,512]{2,1,0:...) while((s32[]{:T(128)}, f32[512,2048]{1,0:T(8,128)}, ...), condition=%wide.region_4.5_spmd.clone, body=%wide.region_2.4_spmd.clone.sunk | while | flops 18154459136 | bytes 265054288 | solution.py:169
  33.6 1.3 fusion.66
  34.9 0.8 gather_fusion.1
  35.7 0.8 gather_fusion.3
  36.4 0.6 compare_select_fusion.13
  37.1 0.0 copy-start.16
  37.1 0.0 copy-done.18
  37.1 0.7 gather_fusion.2
  37.8 0.0 copy-start.12
  37.8 2.7 gather_fusion
  40.5 1.6 multiply_multiply_fusion.2
  42.1 2.0 gather_fusion.4
  44.1 0.0 copy-done.16
  44.1 0.0 copy-done.12
  44.1 0.0 slice-start
  44.1 7.0 %fusion.63 = f32[64,16,2048]{2,1,0:T(8,128)} fusion(bf16[512,2048]{1,0:T(8,128)(2,1)S(1)} %get-tuple-element.327, bf16[64,16,512]{2,1,0:T(8,128)(2,1)} %gather_fusion, pred[64]{0:T(512)(128)(4,1)S(1)} %get-tuple-element.282), kind=kOutput, calls=%fused_computation.21.clone.1 | convolution fusion | flops 2148007936 | bytes 11534400 | tf_op jit(solution)/shard_map/while/body/dot_general | solution.py:84
  51.1 0.0 copy-done.11
  51.1 0.0 copy-done.14
  51.1 9.8 %fusion.65 = f32[64,16,1024]{2,1,0:T(8,128)} fusion(bf16[1024,2048]{1,0:T(8,128)(2,1)S(1)} %copy-done.11, f32[64,16,2048]{2,1,0:T(8,128)} %fusion.63, f32[64,2048]{1,0:T(8,128)S(1)} %copy-done.14), kind=kOutput, calls=%fused_computation.16.clone.1 | convolution fusion | flops 4299161600 | bytes 17301504 | tf_op jit(solution)/shard_map/while/body/dot_general | solution.py:91
  60.9 0.0 slice-done
  60.9 0.0 slice-done.1
  61.0 0.0 copy-start.15
  61.0 9.4 %bitcast_add_fusion.3 = f32[1024,2048]{1,0:T(8,128)S(1)} fusion(f32[1024,2048]{1,0:T(8,128)S(1)} %bitcast.78, f32[64,16,1024]{2,1,0:T(8,128)} %fusion.65, f32[64]{0:T(128)S(1)} %compare_select_fusion.13, f32[64,16,2048]{2,1,0:T(8,128)} %fusion.63, f32[64,2048]{1,0:T(8,128)S(1)} %copy-done.14, bf16[64,16,1024]{2,1,0:T(8,128)(2,1)S(1)} %copy-done.9, ...), kind=kOutput, calls=%fused_computation.7.clone.1 | convolution fusion | flops 4306501632 | bytes 31981888 | tf_op jit(solution)/shard_map/while/body/dot_general | solution.py:102
  70.4 17.4 %multiply_reduce_fusion.2 = (f32[64,2048]{1,0:T(8,128)S(1)}, f32[64,16,2048]{2,1,0:T(8,128)}) fusion(f32[64,16,2048]{2,1,0:T(8,128)} %fusion.63, f32[64,2048]{1,0:T(8,128)S(1)} %copy-done.15, bf16[1024,2048]{1,0:T(8,128)(2,1)} %get-tuple-element.329, f32[64,16,1024]{2,1,0:T(8,128)} %fusion.65, f32[64]{0:T(128)S(1)} %compare_select_fusion.13, ...), kind=kOutput, calls=%fused_computation.8.clone.1 | convolution fusion | flops 4306370560 | bytes 28311872 | tf_op jit(solution)/shard_map/while/body/dot_general | solution.py:105
  87.8 0.0 copy-done.8
  87.8 0.0 copy-start.13
  87.9 0.0 copy-start.17
  87.9 6.3 %fusion.67 = f32[512,2048,1]{1,0,2:T(8,128)S(1)} fusion(f32[64,16,2048]{2,1,0:T(8,128)} %get-tuple-element.285, f32[64,2048]{1,0:T(8,128)S(1)} %copy-done.14, bf16[64,16,512]{2,1,0:T(8,128)(2,1)S(1)} %copy-done.10, pred[64]{0:T(512)(128)(4,1)S(1)} %get-tuple-element.282), kind=kOutput, calls=%fused_computation.11.clone.1 | convolution fusion | flops 2152202240 | bytes 14155840 | tf_op jit(solution)/shard_map/while/body/dot_general | solution.py:115
  94.1 0.0 copy-done.2
  94.2 0.0 copy-done.13
  94.2 0.0 copy-done.17
  94.2 0.0 copy-start.1
  94.2 0.0 copy-start.5
  94.2 0.0 copy-start.7
  94.2 3.2 fusion.68
  97.4 0.0 copy-start.3
  97.4 2.0 copy-done.3
  99.4 0.0 copy-done.1
  99.6 9.4 %reshape_reshape.7 = f32[64,32768]{1,0:T(8,128)} reshape(f32[1024,2048]{1,0:T(8,128)} %get-tuple-element.378) | data formatting | bytes 16777216 | tf_op jit(solution)/shard_map/reshape;reshape | solution.py:24
  109.0 5.0 %reshape_reshape.6 = f32[64,16384]{1,0:T(8,128)} reshape(f32[512,2048]{1,0:T(8,128)} %get-tuple-element.377) | data formatting | bytes 8388608 | tf_op jit(solution)/shard_map/reshape;reshape | solution.py:24
  114.0 10.0 %pad_maximum_fusion = f32[64,49152]{1,0:T(8,128)} fusion(f32[64,32768]{1,0:T(8,128)} %reshape_reshape.7, f32[64,16384]{1,0:T(8,128)} %reshape_reshape.6), kind=kLoop, calls=%fused_computation.59 | loop fusion | flops 3145728 | bytes 25165824 | tf_op jit(solution)/shard_map/concatenate | solution.py:24
  124.0 11.8 %reshape.124 = f32[24576,128]{1,0:T(8,128)} reshape(f32[64,49152]{1,0:T(8,128)} %pad_maximum_fusion) | data formatting | bytes 25165824 | tf_op jit(solution)/shard_map/reshape | solution.py:26
  135.8 0.0 reduce-scatter.2.cloned.1.call-update
  135.8 163.6 %reduce-scatter.2.cloned.1.call-done = f32[384,128]{1,0:T(8,128)} async-done(((f32[24576,128]{1,0:T(8,128)}), f32[384,128]{1,0:T(8,128)}) %reduce-scatter.2.cloned.1.call-update) | async-done | bytes 196624 | tf_op jit(solution)/shard_map/reduce_scatter | solution.py:27
  299.4 0.9 slice.24
  300.3 0.8 slice.23
  301.3 0.1 copy.21
  301.3 10.3 %all_to_all.5 = f32[4,24,512]{2,1,0:T(8,128)S(1)} all-to-all(f32[4,24,512]{2,1,0:T(8,128)S(1)} %copy.21), channel_id=1, replica_groups=mesh['dp'=64,'mp'=4] {'mp'}, dimensions={0} | all-to-all | bytes 393216 | tf_op jit(solution)/shard_map/all_to_all | solution.py:37
  311.7 0.6 split.8
  312.3 0.6 split.9
  (30 shorter events, 0.2 us)
Async XLA Ops:
  7.2 9.2 %copy-start = (bf16[2,512]{1,0:T(2,128)(2,1)S(1)}, bf16[2,512]{1,0:T(2,128)(2,1)}, u32[]{:S(2)}) copy-start(bf16[2,512]{1,0:T(2,128)(2,1)} %param.9) | copy-start | bytes 6148
  7.2 292.2 %reduce-scatter.2.cloned.1.call-start = ((), (), s32[]{:S(2)}) async-start(), calls=%async_computation.2 | async-start | bytes 12779520 | tf_op jit(solution)/shard_map/reduce_scatter | solution.py:27
  28.0 5.6 %copy-start.4 = (bf16[2,256,1024]{2,1,0:T(8,128)(2,1)S(1)}, bf16[2,256,1024]{2,1,0:T(8,128)(2,1)}, u32[]{:S(2)}) copy-start(bf16[2,256,1024]{2,1,0:T(8,128)(2,1)} %param.12) | copy-start | bytes 3145732
  28.0 5.6 %copy-start.6 = (bf16[512,2048]{1,0:T(8,128)(2,1)S(1)}, bf16[512,2048]{1,0:T(8,128)(2,1)}, u32[]{:S(2)}) copy-start(bf16[512,2048]{1,0:T(8,128)(2,1)} %param.14) | copy-start | bytes 6291460
  33.6 3.5 %copy-start.18 = (s32[96]{0:T(128)}, s32[96]{0:T(128)S(1)}, u32[]{:S(2)}) copy-start(s32[96]{0:T(128)S(1)} %get-tuple-element.325) | copy-start | bytes 1156 | tf_op jit(solution)/shard_map/while
  37.1 7.0 %copy-start.16 = (pred[64]{0:T(512)(128)(4,1)}, pred[64]{0:T(512)(128)(4,1)S(1)}, u32[]{:S(2)}) copy-start(pred[64]{0:T(512)(128)(4,1)S(1)} %compare_and_fusion.5) | copy-start | bytes 196 | tf_op jit(solution)/shard_map/while
  37.8 6.3 %copy-start.12 = (bf16[64,512]{1,0:T(8,128)(2,1)}, bf16[64,512]{1,0:T(8,128)(2,1)S(1)}, u32[]{:S(2)}) copy-start(bf16[64,512]{1,0:T(8,128)(2,1)S(1)} %gather_fusion.2) | copy-start | bytes 196612 | tf_op jit(solution)/shard_map/while
  44.1 7.0 %copy-start.11 = (bf16[1024,2048]{1,0:T(8,128)(2,1)S(1)}, bf16[1024,2048]{1,0:T(8,128)(2,1)}, u32[]{:S(2)}) copy-start(bf16[1024,2048]{1,0:T(8,128)(2,1)} %get-tuple-element.329) | copy-start | bytes 12582916 | tf_op jit(solution)/shard_map/while
  44.1 7.0 %copy-start.14 = (f32[64,2048]{1,0:T(8,128)S(1)}, f32[64,2048]{1,0:T(8,128)}, u32[]{:S(2)}) copy-start(f32[64,2048]{1,0:T(8,128)} %get-tuple-element.284) | copy-start | bytes 1572868 | tf_op jit(solution)/shard_map/while
  44.1 16.8 %slice-start = ((s8[8388608]{0:T(1024)(128)(4,1)}), s8[4194304]{0:T(1024)(128)(4,1)S(1)}, s32[]{:S(2)}) async-start(s8[8388608]{0:T(1024)(128)(4,1)} %bitcast.77), calls=%async_computation.3 | async-start | bytes 8388608 | tf_op jit(solution)/shard_map/while
  51.1 9.8 %slice-start.1 = ((s8[8388608]{0:T(1024)(128)(4,1)}), s8[4194304]{0:T(1024)(128)(4,1)S(1)}, s32[]{:S(2)}) async-start(s8[8388608]{0:T(1024)(128)(4,1)} %bitcast.77), calls=%async_computation.4 | async-start | bytes 8388608 | tf_op jit(solution)/shard_map/while
  51.1 9.8 %copy-start.9 = (bf16[64,16,1024]{2,1,0:T(8,128)(2,1)S(1)}, bf16[64,16,1024]{2,1,0:T(8,128)(2,1)}, u32[]{:S(2)}) copy-start(bf16[64,16,1024]{2,1,0:T(8,128)(2,1)} %gather_fusion.4) | copy-start | bytes 6291460 | tf_op jit(solution)/shard_map/while
  61.0 9.5 %copy-start.15 = (f32[64,2048]{1,0:T(8,128)S(1)}, f32[64,2048]{1,0:T(8,128)}, u32[]{:S(2)}) copy-start(f32[64,2048]{1,0:T(8,128)} %get-tuple-element.283) | copy-start | bytes 1572868 | tf_op jit(solution)/shard_map/while
  70.4 17.4 %copy-start.8 = (f32[1024,2048]{1,0:T(8,128)}, f32[1024,2048]{1,0:T(8,128)S(1)}, u32[]{:S(2)}) copy-start(f32[1024,2048]{1,0:T(8,128)S(1)} %bitcast_add_fusion.3) | copy-start | bytes 25165828 | tf_op jit(solution)/shard_map/while
  70.4 17.4 %copy-start.10 = (bf16[64,16,512]{2,1,0:T(8,128)(2,1)S(1)}, bf16[64,16,512]{2,1,0:T(8,128)(2,1)}, u32[]{:S(2)}) copy-start(bf16[64,16,512]{2,1,0:T(8,128)(2,1)} %gather_fusion) | copy-start | bytes 3145732 | tf_op jit(solution)/shard_map/while
  87.8 6.3 %copy-start.2 = (f32[512,2048]{1,0:T(8,128)S(1)}, f32[512,2048]{1,0:T(8,128)}, u32[]{:S(2)}) copy-start(f32[512,2048]{1,0:T(8,128)} %get-tuple-element.305) | copy-start | bytes 12582916 | tf_op jit(solution)/shard_map/while
  87.8 6.3 %copy-start.13 = (bf16[64,512]{1,0:T(8,128)(2,1)S(1)}, bf16[64,512]{1,0:T(8,128)(2,1)}, u32[]{:S(2)}) copy-start(bf16[64,512]{1,0:T(8,128)(2,1)} %copy-done.12) | copy-start | bytes 196612 | tf_op jit(solution)/shard_map/while
  87.9 6.3 %copy-start.17 = (pred[64]{0:T(512)(128)(4,1)S(1)}, pred[64]{0:T(512)(128)(4,1)}, u32[]{:S(2)}) copy-start(pred[64]{0:T(512)(128)(4,1)} %copy-done.16) | copy-start | bytes 196 | tf_op jit(solution)/shard_map/while
  94.2 5.2 %copy-start.1 = (bf16[2,512]{1,0:T(2,128)(2,1)S(1)}, bf16[2,512]{1,0:T(2,128)(2,1)}, u32[]{:S(2)}) copy-start(bf16[2,512]{1,0:T(2,128)(2,1)} %get-tuple-element.356) | copy-start | bytes 6148 | tf_op jit(solution)/shard_map/while
  94.2 5.2 %copy-start.5 = (bf16[2,256,1024]{2,1,0:T(8,128)(2,1)S(1)}, bf16[2,256,1024]{2,1,0:T(8,128)(2,1)}, u32[]{:S(2)}) copy-start(bf16[2,256,1024]{2,1,0:T(8,128)(2,1)} %get-tuple-element.375) | copy-start | bytes 3145732 | tf_op jit(solution)/shard_map/while
  94.2 5.2 %copy-start.7 = (bf16[512,2048]{1,0:T(8,128)(2,1)S(1)}, bf16[512,2048]{1,0:T(8,128)(2,1)}, u32[]{:S(2)}) copy-start(bf16[512,2048]{1,0:T(8,128)(2,1)} %get-tuple-element.395) | copy-start | bytes 6291460 | tf_op jit(solution)/shard_map/while
  94.2 5.2 %copy-start.19 = (s32[96]{0:T(128)S(1)}, s32[96]{0:T(128)}, u32[]{:S(2)}) copy-start(s32[96]{0:T(128)} %copy-done.18) | copy-start | bytes 1156 | tf_op jit(solution)/shard_map/while
  97.4 2.0 copy-start.3
Sparse Core Ops, SparseCore 0:
  135.9 163.4 reduce-scatter.1
where the time goes:
time: 321 us; the launch traced here: 320 us
  waiting for transfers between devices  164 us (51%)
  matrix products  69.9 us (22%)
  local copies, waits for them, and re-layouts  44.4 us (14%)
  other arithmetic  16.2 us (5%)
  between operations  14.7 us (5%)
  blocking collectives  10.3 us (3%)
    reduce_scatter x1, waiting for transfers between devices, sum_together(): lax.psum_scatter(lines, axis, tiled=True).reshape(-1)  164 us
    dot_general x1, matrix products, block_terms(): jnp.dot(jac_grad, decoder_weight, preferred_element_type=jnp.float32)  17.4 us
    another operation x2, local copies, waits for them, and re-layouts, sum_together(): lines = jnp.concatenate([b.reshape(devices, -1) for b in pieces], axis=1)  14.3 us
    reshape x1, local copies, waits for them, and re-layouts, sum_together(): jnp.pad(lines, ((0, 0), (0, width * 128 - lines.shape[1]))).reshape(-1, 128)  11.8 us
    all_to_all x1, blocking collectives, sent_and_summed(): lax.all_to_all(pieces, axis, split_axis=0, concat_axis=0, tiled=True)  10.3 us
    concatenate x1, other arithmetic, sum_together(): lines = jnp.concatenate([b.reshape(devices, -1) for b in pieces], axis=1)  10 us
    dot_general x1, matrix products, block_terms(): lax.dot_general(pushed, decoder_weight, contract_last, preferred_element_...  9.8 us
    dot_general x1, matrix products, block_terms(): lax.dot_general(jac_grad, pushed, contract_first, preferred_element_type=...  9.44 us
  transfers between devices with their start and end apart: 1, of which 1 were waited for; matrix products, arithmetic and copies ran while one was open for 0% of the time, Pallas kernels for 0%

commit v1 on v0

v1 whole, which is shorter than its diff:
```python
import functools
import math

import jax
import jax.numpy as jnp
from jax import lax
from jax.experimental import pallas as pl
from jax.experimental.pallas import tpu as pltpu
from jax.sharding import PartitionSpec as P

F32 = jnp.float32
BF16 = jnp.bfloat16
S16 = jnp.int16
BLK = 16
EXTRA = 16
KT = 256
COLS = 512
DEC = 16
ENC = 8
TOP = 32700.0
TINY = 1e-30
MIB = 1 << 20

NN = (((1,), (0,)), ((), ()))
NT = (((1,), (1,)), ((), ()))


def dot(a, b, dims=NN):
    return lax.dot_general(a, b, dims, preferred_element_type=F32)


def message_rows(blocks):
    return 16 + DEC * blocks + max(16, ENC * blocks)


def exponents(largest):
    return jnp.floor(jnp.log(jnp.maximum(largest, TINY)) * (1.0 / math.log(2.0))) + 1.0


def power(e):
    return jnp.exp(e * math.log(2.0))


def twice(v, rows):
    return jnp.concatenate([v] * (rows // 8), axis=0) if rows > 8 else v


def coded(x, mult):
    return jnp.round(x * twice(mult, x.shape[0])).astype(jnp.int32).astype(S16)


def fold_max(best, x):
    for r in range(0, x.shape[0], 8):
        best = jnp.maximum(best, jnp.abs(x[r : r + 8]))
    return best


def write_scales(msg, best_dec, best_enc):
    e_dec, e_enc = exponents(best_dec), exponents(best_enc)
    both = jnp.concatenate([e_dec, e_enc], axis=0)
    msg[0:16, :] = both.astype(jnp.int32).astype(S16)
    return power(-e_dec) * TOP, power(-e_enc) * TOP


def read_scales(msg):
    both = msg[0:16, :].astype(jnp.int32).astype(F32)
    s = power(both) * (1.0 / TOP)
    return s[0:8], s[8:16]


def plain(q, mult):
    return q.astype(jnp.int32).astype(F32) * twice(mult, q.shape[0])


def rows_loop(count, step, body, init):
    n = count // step
    if n == 1:
        return body(0, init)
    unroll = 4 if n % 4 == 0 else (2 if n % 2 == 0 else 1)

    def it(i, carry):
        for u in range(unroll):
            carry = body(pl.multiple_of((i * unroll + u) * step, step), carry)
        return carry

    return lax.fori_loop(0, n // unroll, it, init)


def encode_rows(src, src_start, count, msg, msg_start, mult):
    step = min(16, count)

    def body(o, carry):
        x = src[pl.ds(src_start + o, step), :]
        msg[pl.ds(msg_start + o, step), :] = coded(x, mult)
        return carry

    rows_loop(count, step, body, 0)


def step_kernel(spec, n_msgs, sizes, *refs):
    groups, keep_blocks, out_sizes = spec
    state_dec, state_enc = refs[0], refs[1]
    msgs = refs[2 : 2 + n_msgs]
    outs = refs[2 + n_msgs :]
    new_dec, new_enc = outs[0], outs[1]
    sent = outs[2 : 2 + len(out_sizes)]
    hold_dec, hold_enc = outs[2 + len(out_sizes) :] if out_sizes else (None, None)
    scales = [read_scales(m) for m in msgs]
    zero = jnp.zeros((8, COLS), F32)
    best = [[zero, zero] for _ in out_sizes]
    pending = []
    held = 0
    for start, blocks, arrived, dest in groups:
        for part, per, state, new, hold in (
            (0, DEC, state_dec, new_dec, hold_dec),
            (1, ENC, state_enc, new_enc, hold_enc),
        ):
            count = per * blocks
            step = min(16, count)

            def value(o, part=part, per=per, state=state, start=start, arrived=arrived, step=step):
                x = state[pl.ds(start * per + o, step), :]
                for m, at in arrived:
                    base = 16 + (DEC * sizes[m] if part else 0) + per * at
                    x = x + plain(msgs[m][pl.ds(base + o, step), :], scales[m][part])
                return x

            if dest[0] == "keep":
                at = dest[1] * per

                def body(o, carry, value=value, new=new, at=at, step=step):
                    new[pl.ds(at + o, step), :] = value(o)
                    return carry

                rows_loop(count, step, body, 0)
            else:
                at = held * per

                def body(o, carry, value=value, hold=hold, at=at, step=step):
                    x = value(o)
                    hold[pl.ds(at + o, step), :] = x
                    return fold_max(carry, x)

                best[dest[1]][part] = rows_loop(count, step, body, best[dest[1]][part])
        if dest[0] == "send":
            pending.append((held, blocks, dest[1], dest[2]))
            held += blocks
    mults = [write_scales(sent[j], *best[j]) for j in range(len(out_sizes))]
    for at, blocks, j, to in pending:
        encode_rows(hold_dec, at * DEC, blocks * DEC, sent[j], 16 + to * DEC, mults[j][0])
        base = 16 + out_sizes[j] * DEC + to * ENC
        if blocks == 1:
            x = coded(hold_enc[at * ENC : at * ENC + 8, :], mults[j][1])
            sent[j][base : base + 8, :] = x
            sent[j][base + 8 : base + 16, :] = jnp.zeros((8, COLS), S16)
        else:
            encode_rows(hold_enc, at * ENC, blocks * ENC, sent[j], base, mults[j][1])


def reduce_step(name, groups, keep_blocks, in_sizes, out_sizes, state, msgs):
    held = sum(g[1] for g in groups if g[3][0] == "send")
    out_shape = [
        jax.ShapeDtypeStruct((keep_blocks * DEC, COLS), F32),
        jax.ShapeDtypeStruct((keep_blocks * ENC, COLS), F32),
    ] + [jax.ShapeDtypeStruct((message_rows(n), COLS), S16) for n in out_sizes]
    scratch = []
    if out_sizes:
        scratch = [pltpu.VMEM((held * DEC, COLS), F32), pltpu.VMEM((held * ENC, COLS), F32)]
    vmem = pl.BlockSpec(memory_space=pltpu.VMEM)
    outs = pl.pallas_call(
        functools.partial(step_kernel, (groups, keep_blocks, out_sizes), len(msgs), in_sizes),
        out_shape=out_shape,
        in_specs=[vmem] * (2 + len(msgs)),
        out_specs=[vmem] * len(out_shape),
        scratch_shapes=scratch,
        compiler_params=pltpu.CompilerParams(vmem_limit_bytes=40 * MIB),
        name=name,
    )(*state, *msgs)
    return outs[:2], outs[2:]


def step_specs():
    core = []
    for h in (0, 1):
        core.append((h * 64, 32, ((0, h * 64),), ("keep", h * 32)))
        core.append((h * 64 + 32, 32, ((0, h * 64 + 32),), ("send", h, 0)))
    a1 = []
    for h in (0, 1):
        a1.append((h * 32, 16, ((h, 0),), ("keep", h * 16)))
        a1.append((h * 32 + 16, 16, ((h, 16),), ("send", h, 0)))
    a2 = []
    for h in (0, 1):
        for b in range(4):
            dest = ("keep", h * 4) if b == 0 else ("send", b - 1, h * 4)
            a2.append((h * 16 + b * 4, 4, ((h, b * 4),), dest))
    b = [
        (0, 4, tuple((k, 0) for k in range(3)), ("keep", 0)),
        (4, 4, tuple((k, 4) for k in range(3)), ("send", 0, 0)),
    ]
    z1 = [(0, 1, ((0, 0),), ("keep", 0))]
    z1 += [(i, 1, ((0, i),), ("send", i - 1, 0)) for i in (1, 2, 3)]
    z2 = [(0, 1, tuple((k, 0) for k in range(3)), ("keep", 0))]
    return (
        ("core", core, 64, (128,), (32, 32)),
        ("a1", a1, 32, (32, 32), (16, 16)),
        ("a2", a2, 8, (16, 16), (8, 8, 8)),
        ("b", b, 4, (8, 8, 8), (4,)),
        ("z1", z1, 1, (4,), (1, 1, 1)),
        ("z2", z2, 1, (1, 1, 1), ()),
    )


def terms_kernel(
    factor,
    ranks,
    table,
    x_ref,
    y_ref,
    dirs,
    targets,
    enc,
    dec,
    mine_dec,
    mine_enc,
    msg,
    along_s,
    pushed,
    lifted,
    jac,
    cols,
    jac_t,
    cols_t,
    out_dec,
    out_enc,
):
    hidden = enc.shape[1]
    in_width = enc.shape[0]
    out_width = dec.shape[0]
    rmax = dirs.shape[1]
    r0, r1 = ranks[0], ranks[1]
    ends = (EXTRA, pl.multiple_of(EXTRA + r0, BLK))
    tail = pl.multiple_of(EXTRA + rmax + r0, BLK)
    for ref in (pushed, lifted, jac, cols):
        ref[pl.ds(tail, KT), :] = jnp.zeros((KT, ref.shape[1]), BF16)

    def pair(ref):
        v = ref[...].astype(F32)
        odd = lax.broadcasted_iota(jnp.int32, (EXTRA, v.shape[1]), 0) % 2 == 1
        top = jnp.broadcast_to(v[0:1], odd.shape)
        return jnp.where(odd, jnp.broadcast_to(v[1:2], odd.shape), top)

    x16 = pair(x_ref).astype(BF16)
    y16 = pair(y_ref)
    cols[0:EXTRA, :] = x16
    hid = jnp.tanh(dot(x16, enc[...]))
    slopes = 1.0 - hid * hid
    act = hid.astype(BF16)
    pushed[0:EXTRA, :] = act
    row = lax.broadcasted_iota(jnp.int32, (EXTRA, out_width), 0)
    misfit_grad = (factor * (dot(act, dec[...], NT) - y16)).astype(BF16)
    jac[0:EXTRA, :] = jnp.where(row < 2, misfit_grad.astype(F32), 0.0).astype(BF16)
    entered = dot(misfit_grad, dec[...]) * slopes

    sums = []
    for s in (0, 1):
        at = ends[s]
        rank = ranks[s]
        d = dirs[s]
        cols[pl.ds(at, rmax), :] = d
        for n in range(0, hidden, COLS):
            al = dot(d, enc[:, n : n + COLS])
            along_s[:, n : n + COLS] = al
            pushed[pl.ds(at, rmax), n : n + COLS] = (al * slopes[s : s + 1, n : n + COLS]).astype(BF16)
        weight = (factor * BLK) / jnp.full((rmax, COLS), rank, jnp.int32).astype(F32)
        live = lax.broadcasted_iota(jnp.int32, (rmax, COLS), 0) < rank
        weight = jnp.where(live, weight, 0.0)
        p = pushed[pl.ds(at, rmax), :]
        for n in range(0, out_width, COLS):
            im = dot(p, dec[n : n + COLS, :], NT)
            diff = im - targets[s, :, n : n + COLS].astype(F32)
            jac[pl.ds(at, rmax), n : n + COLS] = (diff * weight).astype(BF16)
        j = jac[pl.ds(at, rmax), :]
        curve = []
        for n in range(0, hidden, COLS):
            back = dot(j, dec[:, n : n + COLS])
            sl = slopes[s : s + 1, n : n + COLS]
            lifted[pl.ds(at, rmax), n : n + COLS] = (back * sl).astype(BF16)
            total = jnp.sum(back * along_s[:, n : n + COLS], axis=0, keepdims=True)
            curve.append(-2.0 * hid[s : s + 1, n : n + COLS] * sl * total)
        sums.append(jnp.concatenate(curve, axis=1))
    row = lax.broadcasted_iota(jnp.int32, (EXTRA, hidden), 0)
    sc = jnp.where(row % 2 == 1, jnp.broadcast_to(sums[1], row.shape), jnp.broadcast_to(sums[0], row.shape))
    hi = sc.astype(BF16).astype(F32)
    mid = (sc - hi).astype(BF16).astype(F32)
    low = sc - hi - mid
    ent = entered.astype(BF16).astype(F32)
    rest = jnp.where(row < 6, mid, jnp.where(row < 8, low, 0.0))
    lifted[0:EXTRA, :] = jnp.where(row < 2, ent, jnp.where(row < 4, hi, rest)).astype(BF16)

    passes = (EXTRA + r0 + r1 + KT - 1) // KT
    for many in (1, 2, 3):

        @pl.when(passes == many)
        def _(many=many):
            depth = KT * many
            for k in range(0, depth, KT):
                for n in range(0, out_width, KT):
                    jac_t[n : n + KT, k : k + KT] = jac[k : k + KT, n : n + KT].T
                for n in range(0, in_width, KT):
                    cols_t[n : n + KT, k : k + KT] = cols[k : k + KT, n : n + KT].T

            def column_block(xb, carry):
                at = pl.ds(pl.multiple_of(xb * COLS, COLS), COLS)
                pb = pushed[0:depth, at]
                for n in range(0, out_width, KT):
                    g = dot(jac_t[n : n + KT, 0:depth], pb)
                    for r in range(0, KT, DEC):
                        to = table[xb * 64 + (n + r) // DEC]
                        out_dec[pl.ds(pl.multiple_of(to * DEC, DEC), DEC), :] = g[r : r + DEC]
                lb = lifted[0:depth, at]
                for n in range(0, in_width, KT):
                    g = dot(cols_t[n : n + KT, 0:depth], lb)
                    for r in range(0, KT, ENC):
                        to = table[xb * 64 + (n + r) // ENC]
                        out_enc[pl.ds(pl.multiple_of(to * ENC, ENC), ENC), :] = g[r : r + ENC]
                return carry

            lax.fori_loop(0, hidden // COLS, column_block, 0)

    blocks = mine_dec.shape[0] // DEC
    half_dec, half_enc = blocks * DEC, blocks * ENC

    def copy_and_max(src, dst, half):
        def body(o, best):
            dst[pl.ds(o, 16), :] = src[pl.ds(o, 16), :]
            return fold_max(best, src[pl.ds(half + o, 16), :])

        return rows_loop(half, 16, body, jnp.zeros((8, COLS), F32))

    best_dec = copy_and_max(out_dec, mine_dec, half_dec)
    best_enc = copy_and_max(out_enc, mine_enc, half_enc)
    m_dec, m_enc = write_scales(msg, best_dec, best_enc)
    encode_rows(out_dec, half_dec, half_dec, msg, 16, m_dec)
    encode_rows(out_enc, half_enc, half_enc, msg, 16 + half_dec, m_enc)


def own_terms(factor, ranks, table, x, y, dirs, targets, enc, dec):
    rmax = dirs.shape[1]
    in_width, hidden = enc.shape
    out_width = dec.shape[0]
    rows = EXTRA + 2 * rmax + KT
    depth = -(-(EXTRA + 2 * rmax) // KT) * KT
    blocks = (out_width // DEC) * (hidden // COLS) // 2
    vmem = pl.BlockSpec(memory_space=pltpu.VMEM)
    smem = pl.BlockSpec(memory_space=pltpu.SMEM)
    outs = pl.pallas_call(
        functools.partial(terms_kernel, factor),
        out_shape=[
            jax.ShapeDtypeStruct((blocks * DEC, COLS), F32),
            jax.ShapeDtypeStruct((blocks * ENC, COLS), F32),
            jax.ShapeDtypeStruct((message_rows(blocks), COLS), S16),
        ],
        in_specs=[smem, smem] + [vmem] * 6,
        out_specs=[vmem] * 3,
        scratch_shapes=[
            pltpu.VMEM((rmax, hidden), F32),
            pltpu.VMEM((rows, hidden), BF16),
            pltpu.VMEM((rows, hidden), BF16),
            pltpu.VMEM((rows, out_width), BF16),
            pltpu.VMEM((rows, in_width), BF16),
            pltpu.VMEM((out_width, depth), BF16),
            pltpu.VMEM((in_width, depth), BF16),
            pltpu.VMEM((2 * blocks * DEC, COLS), F32),
            pltpu.VMEM((2 * blocks * ENC, COLS), F32),
        ],
        compiler_params=pltpu.CompilerParams(vmem_limit_bytes=60 * MIB),
        name="terms",
    )(ranks, table, x, y, dirs, targets, enc, dec)
    return outs[:2], outs[2:]


def place_table(z, y, core, x):
    i = jnp.arange(256, dtype=jnp.int32)
    xb, zb, yb, cb = i // 64, (i // 8) % 8, (i // 2) % 4, i % 2
    odd = (zb ^ z) & 1
    zi = ((zb - (z ^ odd)) & 7) >> 1
    first = cb == 0
    ea = jnp.where(first, xb ^ x, yb ^ y)
    eb = jnp.where(first, yb - y, xb - x) & 3
    ap = jnp.where(ea == 0, 0, jnp.where(ea == 2, 3, jnp.where((ea == 3) == (odd == 0), 1, 2)))
    group = jnp.where(cb == core, 0, 128)
    return group + odd * 64 + ap * 16 + eb * 4 + zi


def partners(fn):
    pairs = []
    for z in range(8):
        for y in range(4):
            for c in range(2):
                for x in range(4):
                    z2, y2, c2, x2 = fn(z, y, c, x)
                    pairs.append((((z * 4 + y) * 2 + c) * 4 + x, ((z2 * 4 + y2) * 2 + c2) * 4 + x2))
    return pairs


def send(value, fn):
    return lax.ppermute(value, ("dp", "mp"), partners(fn))


def first_axis(flip):
    return lambda z, y, c, x: (z, y, c, x ^ flip) if c == 0 else (z, y ^ flip, c, x)


def second_axis(k):
    return lambda z, y, c, x: (z, (y + k) % 4, c, x) if c == 0 else (z, y, c, (x + k) % 4)


def z_axis(k):
    return lambda z, y, c, x: ((z + k) % 8, y, c, x)


def per_device(sample_inputs, sample_outputs, directions, targets, ranks, enc, dec):
    population = sample_inputs.shape[0] * lax.axis_size("dp") * lax.axis_size("mp")
    factor = 2.0 / math.sqrt(population)
    dp = lax.axis_index("dp")
    x = lax.axis_index("mp")
    z, y, core = dp // 8, (dp // 2) % 4, dp % 2
    table = place_table(z, y, core, x)
    state, msgs = own_terms(
        factor, ranks, table, sample_inputs, sample_outputs, directions, targets, enc, dec
    )
    routes = (
        [lambda z, y, c, x: (z, y, 1 - c, x)],
        [first_axis(1), first_axis(3)],
        [first_axis(3), first_axis(1)],
        [second_axis(k) for k in (1, 2, 3)],
        [lambda z, y, c, x: (z ^ 1, y, c, x)],
        [z_axis(2 * k) for k in (1, 2, 3)],
    )
    for route, (name, groups, keep, in_sizes, out_sizes) in zip(routes, step_specs()):
        arrived = [send(m, fn) for m, fn in zip(msgs, route)]
        state, msgs = reduce_step(name, groups, keep, in_sizes, out_sizes, state, arrived)
    return state[1], state[0]


def solution(mesh):
    both = ("dp", "mp")
    in_specs = (
        P(both, None),
        P(both, None),
        P(both, None, None),
        P(both, None, None),
        P(both),
        P(),
        P(),
    )
    return jax.shard_map(
        per_device,
        mesh=mesh,
        in_specs=in_specs,
        out_specs=(P("dp", "mp"), P("dp", "mp")),
        check_vma=False,
    )
```

time: 321 us -> 89.8 us (0.28)
  waiting for transfers between devices: 164 us -> 36 us
  matrix products: 69.9 us -> 0 us
  local copies, waits for them, and re-layouts: 44.4 us -> 3.78 us
  starting transfers between devices: 0.04 us -> 24.8 us
  Pallas kernels: 0 us -> 23.8 us
  other arithmetic: 16.2 us -> 0.58 us
  between operations: 14.7 us -> 0.71 us
  blocking collectives: 10.3 us -> 0 us
    reduce_scatter x1 -> x0, waiting for transfers between devices: 164 us -> none  [sum_together(): lax.psum_scatter(lines, axis, tiled=True).reshape(-1)]
    dot_general x11 -> x0, matrix products: 69.9 us -> none  [the longest x1 17.4 us: block_terms(): jnp.dot(jac_grad, decoder_weight, preferred_element_type=jnp.float32)]
    ppermute x0 -> x12, waiting for transfers between devices: none -> 36 us  [send(): return lax.ppermute(value, ('dp', 'mp'), partners(fn))]
    ppermute x0 -> x12, starting transfers between devices: none -> 24.8 us  [send(): return lax.ppermute(value, ('dp', 'mp'), partners(fn))]
    pallas_call x0 -> x7, Pallas kernels: none -> 23.8 us  [the longest x1 19.2 us: own_terms(): pl.pallas_call(functools.partial(terms_kernel, factor), out_shape=[jax.Sh...]
    another operation x2 -> x0, local copies, waits for them, and re-layouts: 14.3 us -> none  [sum_together(): lines = jnp.concatenate([b.reshape(devices, -1) for b in pieces], axis=1)]
    reshape x1 -> x0, local copies, waits for them, and re-layouts: 11.8 us -> none  [sum_together(): jnp.pad(lines, ((0, 0), (0, width * 128 - lines.shape[1]))).reshape(-1, 128)]
    all_to_all x1 -> x0, blocking collectives: 10.3 us -> none  [sent_and_summed(): lax.all_to_all(pieces, axis, split_axis=0, concat_axis=0, tiled=True)]
  transfers between devices with their start and end apart: 1 -> 12, of which waited for: 1 -> 10; matrix products, arithmetic and copies ran while one was open for 0% -> 0% of each run, Pallas kernels for 0% -> 0%
where the time goes in v1:
time: 89.8 us; the launch traced here: 89.7 us
  waiting for transfers between devices  36 us (40%)
  starting transfers between devices  24.8 us (28%)
  Pallas kernels  23.8 us (27%)
  local copies, waits for them, and re-layouts  3.78 us (4%)
    ppermute x12, waiting for transfers between devices, send(): return lax.ppermute(value, ('dp', 'mp'), partners(fn))  36 us
    ppermute x12, starting transfers between devices, send(): return lax.ppermute(value, ('dp', 'mp'), partners(fn))  24.8 us
    pallas_call x1, Pallas kernels, own_terms(): pl.pallas_call(functools.partial(terms_kernel, factor), out_shape=[jax.Sh...  19.2 us
    pallas_call x6, Pallas kernels, reduce_step(): pl.pallas_call(functools.partial(step_kernel, (groups, keep_blocks, out_s...  4.58 us
    unnamed x4, local copies, waits for them, and re-layouts  3.78 us
  transfers between devices with their start and end apart: 12, of which 10 were waited for; matrix products, arithmetic and copies ran while one was open for 0% of the time, Pallas kernels for 0%

profile of v1, /device:TPU:8, one launch (start us, length us, event | category | flops | bytes accessed | tf_op | source)
XLA Modules:
  0.0 89.7 jit_solution(4486717505354668727)
XLA Ops:
  0.7 0.6 fusion.3.table
  1.2 19.2 %terms.1 = (f32[2048,512]{1,0:T(8,128)}, f32[1024,512]{1,0:T(8,128)}, s16[3088,512]{1,0:T(8,128)(2,1)}) custom-call(s32[2]{0:T(128)} %ranks.1, s32[256]{0:T(256)} %fusion.3.table, bf16[2,512]{1,0:T(2,128)(2,1)} %x_ref.1, bf16[2,1024]{1,0:T(2,128)(2,1)} %y_ref.1, bf16[2,256,512]{2,1,0:T(8,128)(2,1)} %dirs.1, bf16[2,256,1024]{2,1,0:T(8,128)(2,1)} %targets.1, ...), custom_call_target="tpu_custom_call" | custom-call | tf_op jit(solution)/shard_map/terms/pallas_call | solution.py:356
  20.5 0.0 collective-permute-start
  20.5 5.9 %collective-permute-done.refs_2_ = s16[3088,512]{1,0:T(8,128)(2,1)S(1)} collective-permute-done((s16[3088,512]{1,0:T(8,128)(2,1)}, s16[3088,512]{1,0:T(8,128)(2,1)S(1)}, u32[]{:S(2)}, u32[]{:S(2)}) %collective-permute-start) | collective-permute-done | bytes 3162144 | tf_op jit(solution)/shard_map/ppermute | solution.py:407
  26.4 0.0 copy-start
  26.4 2.2 %copy-done = f32[2048,512]{1,0:T(8,128)S(1)} copy-done((f32[2048,512]{1,0:T(8,128)S(1)}, f32[2048,512]{1,0:T(8,128)}, u32[]{:S(2)}) %copy-start) | copy-done | bytes 4194328
  28.6 0.0 copy-start.1
  28.6 1.6 %copy-done.1 = f32[1024,512]{1,0:T(8,128)S(1)} copy-done((f32[1024,512]{1,0:T(8,128)S(1)}, f32[1024,512]{1,0:T(8,128)}, u32[]{:S(2)}) %copy-start.1) | copy-done | bytes 2097176
  30.2 2.0 %core.1 = (f32[1024,512]{1,0:T(8,128)S(1)}, f32[512,512]{1,0:T(8,128)S(1)}, s16[784,512]{1,0:T(8,128)(2,1)S(1)}, s16[784,512]{1,0:T(8,128)(2,1)S(1)}) custom-call(f32[2048,512]{1,0:T(8,128)S(1)} %copy-done, f32[1024,512]{1,0:T(8,128)S(1)} %copy-done.1, s16[3088,512]{1,0:T(8,128)(2,1)S(1)} %collective-permute-done.refs_2_), custom_call_target="tpu_custom_call" | custom-call | tf_op jit(solution)/shard_map/core/pallas_call | solution.py:170
  32.2 1.6 %collective-permute-start.1 = (s16[784,512]{1,0:T(8,128)(2,1)S(1)}, s16[784,512]{1,0:T(8,128)(2,1)S(1)}, u32[]{:S(2)}, u32[]{:S(2)}) collective-permute-start(s16[784,512]{1,0:T(8,128)(2,1)S(1)} %get-tuple-element.33), channel_id=1, source_target_pairs={{0,1},{1,0},{2,3},{3,2},{4,12},{5,13},{6,14},{7,15},{8,9},{9,8},{1... | collective-permute-start | bytes 2408456 | tf_op jit(solution)/shard_map/ppermute | solution.py:407
  33.8 2.1 %collective-permute-start.2 = (s16[784,512]{1,0:T(8,128)(2,1)S(1)}, s16[784,512]{1,0:T(8,128)(2,1)S(1)}, u32[]{:S(2)}, u32[]{:S(2)}) collective-permute-start(s16[784,512]{1,0:T(8,128)(2,1)S(1)} %get-tuple-element.34), channel_id=1, source_target_pairs={{0,3},{1,2},{2,1},{3,0},{4,28},{5,29},{6,30},{7,31},{8,11},{9,10},... | collective-permute-start | bytes 2408456 | tf_op jit(solution)/shard_map/ppermute | solution.py:407
  35.9 8.6 %collective-permute-done.1.refs_2_ = s16[784,512]{1,0:T(8,128)(2,1)S(1)} collective-permute-done((s16[784,512]{1,0:T(8,128)(2,1)S(1)}, s16[784,512]{1,0:T(8,128)(2,1)S(1)}, u32[]{:S(2)}, u32[]{:S(2)}) %collective-permute-start.1) | collective-permute-done | bytes 802848 | tf_op jit(solution)/shard_map/ppermute | solution.py:407
  44.4 2.7 %collective-permute-done.2.refs_3_ = s16[784,512]{1,0:T(8,128)(2,1)S(1)} collective-permute-done((s16[784,512]{1,0:T(8,128)(2,1)S(1)}, s16[784,512]{1,0:T(8,128)(2,1)S(1)}, u32[]{:S(2)}, u32[]{:S(2)}) %collective-permute-start.2) | collective-permute-done | bytes 802848 | tf_op jit(solution)/shard_map/ppermute | solution.py:407
  47.1 1.1 %a1.1 = (f32[512,512]{1,0:T(8,128)S(1)}, f32[256,512]{1,0:T(8,128)S(1)}, s16[400,512]{1,0:T(8,128)(2,1)S(1)}, s16[400,512]{1,0:T(8,128)(2,1)S(1)}) custom-call(f32[1024,512]{1,0:T(8,128)S(1)} %get-tuple-element.31.refs_0_, f32[512,512]{1,0:T(8,128)S(1)} %get-tuple-element.32.refs_1_, s16[784,512]{1,0:T(8,128)(2,1)S(1)} %collective-permute-done.1.refs_2_, ...), custom_call_target="tpu_custom_call" | custom-call | tf_op jit(solution)/shard_map/a1/pallas_call | solution.py:170
  48.2 2.2 %collective-permute-start.3 = (s16[400,512]{1,0:T(8,128)(2,1)S(1)}, s16[400,512]{1,0:T(8,128)(2,1)S(1)}, u32[]{:S(2)}, u32[]{:S(2)}) collective-permute-start(s16[400,512]{1,0:T(8,128)(2,1)S(1)} %get-tuple-element.37), channel_id=1, source_target_pairs={{0,3},{1,2},{2,1},{3,0},{4,28},{5,29},{6,30},{7,31},{8,11},{9,10},... | collective-permute-start | bytes 1228808 | tf_op jit(solution)/shard_map/ppermute | solution.py:407
  50.4 0.0 collective-permute-start.4
  50.4 7.1 %collective-permute-done.3.refs_2_ = s16[400,512]{1,0:T(8,128)(2,1)S(1)} collective-permute-done((s16[400,512]{1,0:T(8,128)(2,1)S(1)}, s16[400,512]{1,0:T(8,128)(2,1)S(1)}, u32[]{:S(2)}, u32[]{:S(2)}) %collective-permute-start.3) | collective-permute-done | bytes 409632 | tf_op jit(solution)/shard_map/ppermute | solution.py:407
  57.5 0.9 collective-permute-done.4.refs_3_
  58.4 0.5 a2.1
  58.9 1.7 %collective-permute-start.5 = (s16[208,512]{1,0:T(8,128)(2,1)S(1)}, s16[208,512]{1,0:T(8,128)(2,1)S(1)}, u32[]{:S(2)}, u32[]{:S(2)}) collective-permute-start(s16[208,512]{1,0:T(8,128)(2,1)S(1)} %get-tuple-element.41), channel_id=1, source_target_pairs={{0,8},{1,9},{2,10},{3,11},{4,5},{5,6},{6,7},{7,4},{8,16},{9,17},{1... | collective-permute-start | bytes 638984 | tf_op jit(solution)/shard_map/ppermute | solution.py:407
  60.5 0.9 %collective-permute-start.6 = (s16[208,512]{1,0:T(8,128)(2,1)S(1)}, s16[208,512]{1,0:T(8,128)(2,1)S(1)}, u32[]{:S(2)}, u32[]{:S(2)}) collective-permute-start(s16[208,512]{1,0:T(8,128)(2,1)S(1)} %get-tuple-element.42), channel_id=1, source_target_pairs={{0,16},{1,17},{2,18},{3,19},{4,6},{5,7},{6,4},{7,5},{8,24},{9,25},... | collective-permute-start | bytes 638984 | tf_op jit(solution)/shard_map/ppermute | solution.py:407
  61.5 2.4 %collective-permute-start.7 = (s16[208,512]{1,0:T(8,128)(2,1)S(1)}, s16[208,512]{1,0:T(8,128)(2,1)S(1)}, u32[]{:S(2)}, u32[]{:S(2)}) collective-permute-start(s16[208,512]{1,0:T(8,128)(2,1)S(1)} %get-tuple-element.43), channel_id=1, source_target_pairs={{0,24},{1,25},{2,26},{3,27},{4,7},{5,4},{6,5},{7,6},{8,0},{9,1},{1... | collective-permute-start | bytes 638984 | tf_op jit(solution)/shard_map/ppermute | solution.py:407
  63.9 0.9 %collective-permute-done.5.refs_2_ = s16[208,512]{1,0:T(8,128)(2,1)S(1)} collective-permute-done((s16[208,512]{1,0:T(8,128)(2,1)S(1)}, s16[208,512]{1,0:T(8,128)(2,1)S(1)}, u32[]{:S(2)}, u32[]{:S(2)}) %collective-permute-start.5) | collective-permute-done | bytes 213024 | tf_op jit(solution)/shard_map/ppermute | solution.py:407
  64.8 3.2 %collective-permute-done.6.refs_3_ = s16[208,512]{1,0:T(8,128)(2,1)S(1)} collective-permute-done((s16[208,512]{1,0:T(8,128)(2,1)S(1)}, s16[208,512]{1,0:T(8,128)(2,1)S(1)}, u32[]{:S(2)}, u32[]{:S(2)}) %collective-permute-start.6) | collective-permute-done | bytes 213024 | tf_op jit(solution)/shard_map/ppermute | solution.py:407
  68.0 1.6 %collective-permute-done.7.refs_4_ = s16[208,512]{1,0:T(8,128)(2,1)S(1)} collective-permute-done((s16[208,512]{1,0:T(8,128)(2,1)S(1)}, s16[208,512]{1,0:T(8,128)(2,1)S(1)}, u32[]{:S(2)}, u32[]{:S(2)}) %collective-permute-start.7) | collective-permute-done | bytes 213024 | tf_op jit(solution)/shard_map/ppermute | solution.py:407
  69.6 0.2 b.1
  69.8 2.0 %collective-permute-start.8 = (s16[112,512]{1,0:T(8,128)(2,1)S(1)}, s16[112,512]{1,0:T(8,128)(2,1)S(1)}, u32[]{:S(2)}, u32[]{:S(2)}) collective-permute-start(s16[112,512]{1,0:T(8,128)(2,1)S(1)} %get-tuple-element.46), channel_id=1, source_target_pairs={{0,32},{1,33},{2,34},{3,35},{4,36},{5,37},{6,38},{7,39},{8,40},{9,... | collective-permute-start | bytes 344072 | tf_op jit(solution)/shard_map/ppermute | solution.py:407
  71.8 2.9 %collective-permute-done.8.refs_2_ = s16[112,512]{1,0:T(8,128)(2,1)S(1)} collective-permute-done((s16[112,512]{1,0:T(8,128)(2,1)S(1)}, s16[112,512]{1,0:T(8,128)(2,1)S(1)}, u32[]{:S(2)}, u32[]{:S(2)}) %collective-permute-start.8) | collective-permute-done | bytes 114720 | tf_op jit(solution)/shard_map/ppermute | solution.py:407
  74.7 0.1 z1.1
  74.8 3.9 %collective-permute-start.9 = (s16[48,512]{1,0:T(8,128)(2,1)S(1)}, s16[48,512]{1,0:T(8,128)(2,1)S(1)}, u32[]{:S(2)}, u32[]{:S(2)}) collective-permute-start(s16[48,512]{1,0:T(8,128)(2,1)S(1)} %get-tuple-element.49), channel_id=1, source_target_pairs={{0,64},{1,65},{2,66},{3,67},{4,68},{5,69},{6,70},{7,71},{8,72},{9,... | collective-permute-start | bytes 147464 | tf_op jit(solution)/shard_map/ppermute | solution.py:407
  78.7 4.9 %collective-permute-start.10 = (s16[48,512]{1,0:T(8,128)(2,1)S(1)}, s16[48,512]{1,0:T(8,128)(2,1)S(1)}, u32[]{:S(2)}, u32[]{:S(2)}) collective-permute-start(s16[48,512]{1,0:T(8,128)(2,1)S(1)} %get-tuple-element.50), channel_id=1, source_target_pairs={{0,128},{1,129},{2,130},{3,131},{4,132},{5,133},{6,134},{7,135},{8... | collective-permute-start | bytes 147464 | tf_op jit(solution)/shard_map/ppermute | solution.py:407
  83.6 3.2 %collective-permute-start.11 = (s16[48,512]{1,0:T(8,128)(2,1)S(1)}, s16[48,512]{1,0:T(8,128)(2,1)S(1)}, u32[]{:S(2)}, u32[]{:S(2)}) collective-permute-start(s16[48,512]{1,0:T(8,128)(2,1)S(1)} %get-tuple-element.51), channel_id=1, source_target_pairs={{0,192},{1,193},{2,194},{3,195},{4,196},{5,197},{6,198},{7,199},{8... | collective-permute-start | bytes 147464 | tf_op jit(solution)/shard_map/ppermute | solution.py:407
  86.8 0.0 collective-permute-done.9.refs_2_
  86.8 0.0 collective-permute-done.10.refs_3_
  86.8 2.3 %collective-permute-done.11.refs_4_ = s16[48,512]{1,0:T(8,128)(2,1)S(1)} collective-permute-done((s16[48,512]{1,0:T(8,128)(2,1)S(1)}, s16[48,512]{1,0:T(8,128)(2,1)S(1)}, u32[]{:S(2)}, u32[]{:S(2)}) %collective-permute-start.11) | collective-permute-done | bytes 49184 | tf_op jit(solution)/shard_map/ppermute | solution.py:407
  89.1 0.7 z2.1
Async XLA Ops:
  20.5 5.9 %collective-permute-start = (s16[3088,512]{1,0:T(8,128)(2,1)}, s16[3088,512]{1,0:T(8,128)(2,1)S(1)}, u32[]{:S(2)}, u32[]{:S(2)}) collective-permute-start(s16[3088,512]{1,0:T(8,128)(2,1)} %get-tuple-element.30), channel_id=1, source_target_pairs={{0,4},{1,5},{2,6},{3,7},{4,0},{5,1},{6,2},{7,3},{8,12},{9,13},{10,... | collective-permute-start | bytes 9486344 | tf_op jit(solution)/shard_map/ppermute | solution.py:407
  26.4 2.2 %copy-start = (f32[2048,512]{1,0:T(8,128)S(1)}, f32[2048,512]{1,0:T(8,128)}, u32[]{:S(2)}) copy-start(f32[2048,512]{1,0:T(8,128)} %get-tuple-element.28.refs_0_) | copy-start | bytes 12582916
  28.6 1.6 %copy-start.1 = (f32[1024,512]{1,0:T(8,128)S(1)}, f32[1024,512]{1,0:T(8,128)}, u32[]{:S(2)}) copy-start(f32[1024,512]{1,0:T(8,128)} %get-tuple-element.29.refs_1_) | copy-start | bytes 6291460
  32.2 12.3 %collective-permute-start.1 = (s16[784,512]{1,0:T(8,128)(2,1)S(1)}, s16[784,512]{1,0:T(8,128)(2,1)S(1)}, u32[]{:S(2)}, u32[]{:S(2)}) collective-permute-start(s16[784,512]{1,0:T(8,128)(2,1)S(1)} %get-tuple-element.33), channel_id=1, source_target_pairs={{0,1},{1,0},{2,3},{3,2},{4,12},{5,13},{6,14},{7,15},{8,9},{9,8},{1... | collective-permute-start | bytes 2408456 | tf_op jit(solution)/shard_map/ppermute | solution.py:407
  33.8 13.4 %collective-permute-start.2 = (s16[784,512]{1,0:T(8,128)(2,1)S(1)}, s16[784,512]{1,0:T(8,128)(2,1)S(1)}, u32[]{:S(2)}, u32[]{:S(2)}) collective-permute-start(s16[784,512]{1,0:T(8,128)(2,1)S(1)} %get-tuple-element.34), channel_id=1, source_target_pairs={{0,3},{1,2},{2,1},{3,0},{4,28},{5,29},{6,30},{7,31},{8,11},{9,10},... | collective-permute-start | bytes 2408456 | tf_op jit(solution)/shard_map/ppermute | solution.py:407
  48.2 9.2 %collective-permute-start.3 = (s16[400,512]{1,0:T(8,128)(2,1)S(1)}, s16[400,512]{1,0:T(8,128)(2,1)S(1)}, u32[]{:S(2)}, u32[]{:S(2)}) collective-permute-start(s16[400,512]{1,0:T(8,128)(2,1)S(1)} %get-tuple-element.37), channel_id=1, source_target_pairs={{0,3},{1,2},{2,1},{3,0},{4,28},{5,29},{6,30},{7,31},{8,11},{9,10},... | collective-permute-start | bytes 1228808 | tf_op jit(solution)/shard_map/ppermute | solution.py:407
  50.4 8.0 %collective-permute-start.4 = (s16[400,512]{1,0:T(8,128)(2,1)S(1)}, s16[400,512]{1,0:T(8,128)(2,1)S(1)}, u32[]{:S(2)}, u32[]{:S(2)}) collective-permute-start(s16[400,512]{1,0:T(8,128)(2,1)S(1)} %get-tuple-element.38), channel_id=1, source_target_pairs={{0,1},{1,0},{2,3},{3,2},{4,12},{5,13},{6,14},{7,15},{8,9},{9,8},{1... | collective-permute-start | bytes 1228808 | tf_op jit(solution)/shard_map/ppermute | solution.py:407
  58.9 5.9 %collective-permute-start.5 = (s16[208,512]{1,0:T(8,128)(2,1)S(1)}, s16[208,512]{1,0:T(8,128)(2,1)S(1)}, u32[]{:S(2)}, u32[]{:S(2)}) collective-permute-start(s16[208,512]{1,0:T(8,128)(2,1)S(1)} %get-tuple-element.41), channel_id=1, source_target_pairs={{0,8},{1,9},{2,10},{3,11},{4,5},{5,6},{6,7},{7,4},{8,16},{9,17},{1... | collective-permute-start | bytes 638984 | tf_op jit(solution)/shard_map/ppermute | solution.py:407
  60.5 7.5 %collective-permute-start.6 = (s16[208,512]{1,0:T(8,128)(2,1)S(1)}, s16[208,512]{1,0:T(8,128)(2,1)S(1)}, u32[]{:S(2)}, u32[]{:S(2)}) collective-permute-start(s16[208,512]{1,0:T(8,128)(2,1)S(1)} %get-tuple-element.42), channel_id=1, source_target_pairs={{0,16},{1,17},{2,18},{3,19},{4,6},{5,7},{6,4},{7,5},{8,24},{9,25},... | collective-permute-start | bytes 638984 | tf_op jit(solution)/shard_map/ppermute | solution.py:407
  61.5 8.1 %collective-permute-start.7 = (s16[208,512]{1,0:T(8,128)(2,1)S(1)}, s16[208,512]{1,0:T(8,128)(2,1)S(1)}, u32[]{:S(2)}, u32[]{:S(2)}) collective-permute-start(s16[208,512]{1,0:T(8,128)(2,1)S(1)} %get-tuple-element.43), channel_id=1, source_target_pairs={{0,24},{1,25},{2,26},{3,27},{4,7},{5,4},{6,5},{7,6},{8,0},{9,1},{1... | collective-permute-start | bytes 638984 | tf_op jit(solution)/shard_map/ppermute | solution.py:407
  69.8 4.9 %collective-permute-start.8 = (s16[112,512]{1,0:T(8,128)(2,1)S(1)}, s16[112,512]{1,0:T(8,128)(2,1)S(1)}, u32[]{:S(2)}, u32[]{:S(2)}) collective-permute-start(s16[112,512]{1,0:T(8,128)(2,1)S(1)} %get-tuple-element.46), channel_id=1, source_target_pairs={{0,32},{1,33},{2,34},{3,35},{4,36},{5,37},{6,38},{7,39},{8,40},{9,... | collective-permute-start | bytes 344072 | tf_op jit(solution)/shard_map/ppermute | solution.py:407
  74.8 11.9 %collective-permute-start.9 = (s16[48,512]{1,0:T(8,128)(2,1)S(1)}, s16[48,512]{1,0:T(8,128)(2,1)S(1)}, u32[]{:S(2)}, u32[]{:S(2)}) collective-permute-start(s16[48,512]{1,0:T(8,128)(2,1)S(1)} %get-tuple-element.49), channel_id=1, source_target_pairs={{0,64},{1,65},{2,66},{3,67},{4,68},{5,69},{6,70},{7,71},{8,72},{9,... | collective-permute-start | bytes 147464 | tf_op jit(solution)/shard_map/ppermute | solution.py:407
  78.7 8.1 %collective-permute-start.10 = (s16[48,512]{1,0:T(8,128)(2,1)S(1)}, s16[48,512]{1,0:T(8,128)(2,1)S(1)}, u32[]{:S(2)}, u32[]{:S(2)}) collective-permute-start(s16[48,512]{1,0:T(8,128)(2,1)S(1)} %get-tuple-element.50), channel_id=1, source_target_pairs={{0,128},{1,129},{2,130},{3,131},{4,132},{5,133},{6,134},{7,135},{8... | collective-permute-start | bytes 147464 | tf_op jit(solution)/shard_map/ppermute | solution.py:407
  83.6 5.5 %collective-permute-start.11 = (s16[48,512]{1,0:T(8,128)(2,1)S(1)}, s16[48,512]{1,0:T(8,128)(2,1)S(1)}, u32[]{:S(2)}, u32[]{:S(2)}) collective-permute-start(s16[48,512]{1,0:T(8,128)(2,1)S(1)} %get-tuple-element.51), channel_id=1, source_target_pairs={{0,192},{1,193},{2,194},{3,195},{4,196},{5,197},{6,198},{7,199},{8... | collective-permute-start | bytes 147464 | tf_op jit(solution)/shard_map/ppermute | solution.py:407

commit v2 on v0

v2 whole, which is shorter than its diff:
```python
import functools
import math

import jax
import jax.numpy as jnp
from jax import lax
from jax.experimental import pallas as pl
from jax.experimental.pallas import tpu as pltpu
from jax.sharding import PartitionSpec as P

F32 = jnp.float32
BF16 = jnp.bfloat16
S16 = jnp.int16
BLK = 16
EXTRA = 16
COLS = 512
PER = (16, 8)
TOP = 32700.0
TINY = 1e-30
MIB = 1 << 20
SIZES = ((256, 256), (416, 512), (528, 640))
ROWS = 784

NN = (((1,), (0,)), ((), ()))
NT = (((1,), (1,)), ((), ()))
VM = pl.BlockSpec(memory_space=pltpu.VMEM)
SM = pl.BlockSpec(memory_space=pltpu.SMEM)
HB = pl.BlockSpec(memory_space=pltpu.HBM)


def dot(a, b, dims=NN):
    return lax.dot_general(a, b, dims, preferred_element_type=F32)


def section_base(sections, index):
    return 16 + sum(PER[p] * n for p, n in sections[:index])


def message_rows(sections):
    rows = section_base(sections, len(sections))
    return -(-rows // 16) * 16


def exponents(largest):
    return jnp.floor(jnp.log(jnp.maximum(largest, TINY)) * (1.0 / math.log(2.0))) + 1.0


def power(e):
    return jnp.exp(e * math.log(2.0))


def twice(v, rows):
    return jnp.concatenate([v] * (rows // 8), axis=0) if rows > 8 else v


def coded(x, mult):
    return jnp.round(x * twice(mult, x.shape[0])).astype(jnp.int32).astype(S16)


def plain(q, mult):
    return q.astype(jnp.int32).astype(F32) * twice(mult, q.shape[0])


def fold_max(best, x):
    for r in range(0, x.shape[0], 8):
        best = jnp.maximum(best, jnp.abs(x[r : r + 8]))
    return best


def write_scales(msg, best):
    es = [exponents(b) for b in best]
    msg[0:16, :] = jnp.concatenate([es[0], es[-1]], axis=0).astype(jnp.int32).astype(S16)
    return [power(-e) * TOP for e in es]


def read_scales(msg):
    s = power(msg[0:16, :].astype(jnp.int32).astype(F32)) * (1.0 / TOP)
    return s[0:8], s[8:16]


def rows_loop(count, step, body, init):
    n = count // step
    if n == 1:
        return body(0, init)
    unroll = 4 if n % 4 == 0 else (2 if n % 2 == 0 else 1)

    def it(i, carry):
        for u in range(unroll):
            carry = body(pl.multiple_of((i * unroll + u) * step, step), carry)
        return carry

    return lax.fori_loop(0, n // unroll, it, init)


def encode_rows(src, src_start, count, msg, msg_start, mult):
    def body(o, carry):
        msg[pl.ds(msg_start + o, 16), :] = coded(src[pl.ds(src_start + o, 16), :], mult)
        return carry

    rows_loop(count, 16, body, 0)


def step_kernel(parts, groups, ins, outs, *refs):
    np_ = len(parts)
    states = dict(zip(parts, refs[:np_]))
    msgs = refs[np_ : np_ + len(ins)]
    rest = refs[np_ + len(ins) :]
    news = dict(zip(parts, rest[:np_]))
    sent = rest[np_ : np_ + len(outs)]
    holds = dict(zip(parts, rest[np_ + len(outs) :]))
    scales = [read_scales(m) for m in msgs]
    zero = jnp.zeros((8, COLS), F32)
    best = [[zero] * len(o) for o in outs]
    pending = []
    held = {p: 0 for p in parts}
    for part, start, blocks, arrived, dest in groups:
        per = PER[part]
        count = per * blocks
        step = min(16, count)

        def value(o, part=part, per=per, start=start, arrived=arrived, step=step):
            x = states[part][pl.ds(start * per + o, step), :]
            for m, at in arrived:
                index = [p for p, _ in ins[m]].index(part)
                base = section_base(ins[m], index) + per * at
                x = x + plain(msgs[m][pl.ds(base + o, step), :], scales[m][index])
            return x

        if dest[0] == "keep":
            to = dest[1] * per

            def body(o, carry, value=value, part=part, to=to, step=step):
                news[part][pl.ds(to + o, step), :] = value(o)
                return carry

            rows_loop(count, step, body, 0)
        else:
            index = [p for p, _ in outs[dest[1]]].index(part)
            to = held[part] * per

            def body(o, carry, value=value, part=part, to=to, step=step):
                x = value(o)
                holds[part][pl.ds(to + o, step), :] = x
                return fold_max(carry, x)

            best[dest[1]][index] = rows_loop(count, step, body, best[dest[1]][index])
            pending.append((part, to, count, dest[1], index, dest[2] * per))
            held[part] += blocks
    mults = [write_scales(sent[j], best[j]) for j in range(len(outs))]
    for part, at, count, j, index, to in pending:
        base = section_base(outs[j], index) + to
        if count < 16:
            x = coded(holds[part][at : at + 8, :], mults[j][index])
            sent[j][base : base + 8, :] = x
            sent[j][base + 8 : base + 16, :] = jnp.zeros((8, COLS), S16)
        else:
            encode_rows(holds[part], at, count, sent[j], base, mults[j][index])


def reduce_step(name, parts, groups, keep, ins, outs, states, msgs):
    scratch = []
    if outs:
        for p in parts:
            held = sum(g[2] for g in groups if g[0] == p and g[4][0] == "send")
            scratch.append(pltpu.VMEM((held * PER[p], COLS), F32))
    out_shape = [jax.ShapeDtypeStruct((keep * PER[p], COLS), F32) for p in parts]
    out_shape += [jax.ShapeDtypeStruct((message_rows(o), COLS), S16) for o in outs]
    got = pl.pallas_call(
        functools.partial(step_kernel, parts, groups, ins, outs),
        out_shape=out_shape,
        in_specs=[VM] * (len(parts) + len(msgs)),
        out_specs=[VM] * len(out_shape),
        scratch_shapes=scratch,
        compiler_params=pltpu.CompilerParams(vmem_limit_bytes=16 * MIB),
        cost_estimate=pl.CostEstimate(flops=int(2e8) * keep, transcendentals=0, bytes_accessed=0),
        name=name,
    )(*states, *msgs)
    return got[: len(parts)], got[len(parts) :]


def core_groups(part):
    groups = []
    for h in (0, 1):
        groups.append((part, h * 64, 32, ((0, h * 64),), ("keep", h * 32)))
        groups.append((part, h * 64 + 32, 32, ((0, h * 64 + 32),), ("send", h, 0)))
    return tuple(groups)


def first_groups(part):
    groups = []
    for h in (0, 1):
        groups.append((part, h * 32, 16, ((h, 0),), ("keep", h * 16)))
        groups.append((part, h * 32 + 16, 16, ((h, 16),), ("send", h, 0)))
    return tuple(groups)


def join_groups():
    groups = []
    for part in (0, 1):
        for h in (0, 1):
            for b in range(4):
                dest = ("keep", h * 4) if b == 0 else ("send", b - 1, h * 4)
                groups.append((part, h * 16 + b * 4, 4, ((part * 2 + h, b * 4),), dest))
    return tuple(groups)


def second_groups():
    groups = []
    for part in (0, 1):
        groups.append((part, 0, 4, tuple((k, 0) for k in range(3)), ("keep", 0)))
        groups.append((part, 4, 4, tuple((k, 4) for k in range(3)), ("send", 0, 0)))
    return tuple(groups)


def half_groups(n):
    groups = []
    for part in (0, 1):
        groups.append((part, 0, n, ((0, 0),), ("keep", 0)))
        groups.append((part, n, n, ((0, n),), ("send", 0, 0)))
    return tuple(groups)


def last_groups():
    return tuple((part, 0, 1, ((0, 0),), ("keep", 0)) for part in (0, 1))


def sections(n):
    return ((0, n), (1, n))


def by_size(total, body):
    low = 0
    for rows, depth in SIZES:

        @pl.when((total > low) & (total <= rows))
        def _(rows=rows, depth=depth):
            body(rows, depth)

        low = rows


def second_rows(rows, r0, width):
    row = lax.broadcasted_iota(jnp.int32, (rows, width), 0)
    return ((row < EXTRA) & (row % 2 == 1)) | (row >= EXTRA + r0)


def spread(second, v0, v1):
    return jnp.where(second, jnp.broadcast_to(v1, second.shape), jnp.broadcast_to(v0, second.shape))


def transposed(src, dst, width, depth):
    for k in range(0, depth, 128):
        for n in range(0, width, 512):
            dst[n : n + 512, k : k + 128] = src[k : k + 128, n : n + 512].T


def products(per, lhs_t, rhs, depth, width, hidden, table, both):
    def column_block(xb, carry):
        b = rhs[0:depth, pl.ds(pl.multiple_of(xb * COLS, COLS), COLS)]
        for n in range(0, width, 256):
            g = dot(lhs_t[n : n + 256, 0:depth], b)
            for r in range(0, 256, per):
                to = table[xb * 64 + (n + r) // per]
                both[pl.ds(pl.multiple_of(to * per, per), per), :] = g[r : r + per]
        return carry

    lax.fori_loop(0, hidden // COLS, column_block, 0)


def encode_other(both, msg):
    half = both.shape[0] // 2
    zero = jnp.zeros((8, COLS), F32)
    best = rows_loop(half, 16, lambda o, c: fold_max(c, both[pl.ds(half + o, 16), :]), zero)
    (mult,) = write_scales(msg, [best])
    encode_rows(both, half, half, msg, 16, mult)


def decoder_kernel(
    factor, ranks, table, x_ref, y_ref, dirs, targets, enc, dec,
    both, msg, jac, along, cols, hid, dec_v,
    enc_v, dirs_v, targets_v, tgt, pushed, jac_t, sems,
):
    in_width, hidden = enc.shape
    out_width = dec.shape[0]
    rmax = dirs.shape[1]
    copies = [
        pltpu.make_async_copy(a, b, sems.at[i])
        for i, (a, b) in enumerate(
            ((dirs, dirs_v), (enc, enc_v), (dec, dec_v), (targets, targets_v))
        )
    ]
    for c in copies:
        c.start()
    r0, r1 = ranks[0], ranks[1]
    at1 = pl.multiple_of(EXTRA + r0, BLK)
    tail = pl.multiple_of(EXTRA + rmax + r0, BLK)
    for ref in (cols, tgt):
        ref[pl.ds(tail, 256), :] = jnp.zeros((256, ref.shape[1]), BF16)

    def pair(ref):
        v = ref[...].astype(F32)
        odd = lax.broadcasted_iota(jnp.int32, (EXTRA, v.shape[1]), 0) % 2 == 1
        return spread(odd, v[0:1], v[1:2]).astype(BF16)

    cols[0:EXTRA, :] = pair(x_ref)
    tgt[0:EXTRA, :] = pair(y_ref)
    copies[0].wait()
    cols[EXTRA : EXTRA + rmax, :] = dirs_v[0]
    cols[pl.ds(at1, rmax), :] = dirs_v[1]
    copies[1].wait()

    def forward(rows, depth):
        second = second_rows(rows, r0, COLS)
        first_row = lax.broadcasted_iota(jnp.int32, (rows, COLS), 0)
        if depth > rows:
            for ref in (pushed, jac):
                ref[rows:depth, :] = jnp.zeros((depth - rows, ref.shape[1]), BF16)

        def hidden_block(n, carry):
            at = pl.ds(pl.multiple_of(n * COLS, COLS), COLS)
            al = dot(cols[0:rows, :], enc_v[:, at])
            along[0:rows, at] = al
            h = jnp.tanh(al[0:EXTRA])
            hid[:, at] = h
            s = 1.0 - h * h
            sl = spread(second, s[0:1], s[1:2])
            pushed[0:rows, at] = (al * sl).astype(BF16)
            pushed[0:EXTRA, at] = h.astype(BF16)
            return carry

        lax.fori_loop(0, hidden // COLS, hidden_block, 0)

        copies[2].wait()
        copies[3].wait()
        tgt[EXTRA : EXTRA + rmax, :] = targets_v[0]
        tgt[pl.ds(at1, rmax), :] = targets_v[1]

        def weight_of(rank):
            return (factor * BLK) / jnp.full((rows, COLS), rank, jnp.int32).astype(F32)

        w = jnp.where(first_row >= EXTRA + r0, weight_of(r1), weight_of(r0))
        w = jnp.where(first_row < EXTRA, jnp.where(first_row < 2, factor, 0.0), w)
        w = jnp.where(first_row < EXTRA + r0 + r1, w, 0.0)

        def output_block(n, carry):
            at = pl.ds(pl.multiple_of(n * COLS, COLS), COLS)
            im = dot(pushed[0:rows, :], dec_v[at, :], NT)
            jac[0:rows, at] = ((im - tgt[0:rows, at].astype(F32)) * w).astype(BF16)
            return carry

        lax.fori_loop(0, out_width // COLS, output_block, 0)
        transposed(jac, jac_t, out_width, depth)
        products(PER[0], jac_t, pushed, depth, out_width, hidden, table, both)

    by_size(EXTRA + r0 + r1, forward)
    encode_other(both, msg)


def encoder_kernel(
    ranks, table, jac, along, cols, hid, dec, both, msg, lifted, cols_t
):
    in_width = cols.shape[1]
    hidden = dec.shape[1]
    r0, r1 = ranks[0], ranks[1]

    def backward(rows, depth):
        second = second_rows(rows, r0, COLS)
        extra_row = lax.broadcasted_iota(jnp.int32, (EXTRA, COLS), 0)
        if depth > rows:
            lifted[rows:depth, :] = jnp.zeros((depth - rows, hidden), BF16)

        def hidden_block(n, carry):
            at = pl.ds(pl.multiple_of(n * COLS, COLS), COLS)
            back = dot(jac[0:rows, :], dec[:, at])
            h = hid[:, at]
            s = 1.0 - h * h
            sl = spread(second, s[0:1], s[1:2])
            up = back * sl
            lifted[0:rows, at] = up.astype(BF16)
            prod = back[EXTRA:] * along[EXTRA:rows, at]
            sec = second[EXTRA:]
            sum0 = jnp.sum(jnp.where(sec, 0.0, prod), axis=0, keepdims=True)
            sum1 = jnp.sum(jnp.where(sec, prod, 0.0), axis=0, keepdims=True)
            sc = -2.0 * h * s * spread(second[0:EXTRA], sum0, sum1)
            hi = sc.astype(BF16).astype(F32)
            mid = (sc - hi).astype(BF16).astype(F32)
            low = sc - hi - mid
            ent = up[0:EXTRA].astype(BF16).astype(F32)
            rest = jnp.where(extra_row < 6, mid, jnp.where(extra_row < 8, low, 0.0))
            fixed = jnp.where(extra_row < 2, ent, jnp.where(extra_row < 4, hi, rest))
            lifted[0:EXTRA, at] = fixed.astype(BF16)
            return carry

        lax.fori_loop(0, hidden // COLS, hidden_block, 0)
        transposed(cols, cols_t, in_width, depth)
        products(PER[1], cols_t, lifted, depth, in_width, hidden, table, both)

    by_size(EXTRA + r0 + r1, backward)
    encode_other(both, msg)


def own_terms(factor, ranks, table, x, y, dirs, targets, enc, dec):
    rmax = dirs.shape[1]
    in_width, hidden = enc.shape
    out_width = dec.shape[0]
    top, depth = SIZES[-1]
    blocks = 128
    shape = jax.ShapeDtypeStruct
    both, msg, jac, along, cols, hid, dec_v = pl.pallas_call(
        functools.partial(decoder_kernel, factor),
        out_shape=[
            shape((2 * blocks * PER[0], COLS), F32),
            shape((message_rows(((0, blocks),)), COLS), S16),
            shape((ROWS, out_width), BF16),
            shape((top, hidden), F32),
            shape((ROWS, in_width), BF16),
            shape((EXTRA, hidden), F32),
            shape(dec.shape, BF16),
        ],
        in_specs=[SM, SM, VM, VM, HB, HB, HB, HB],
        out_specs=[VM] * 7,
        scratch_shapes=[
            pltpu.VMEM(enc.shape, BF16),
            pltpu.VMEM(dirs.shape, BF16),
            pltpu.VMEM(targets.shape, BF16),
            pltpu.VMEM((ROWS, out_width), BF16),
            pltpu.VMEM((ROWS, hidden), BF16),
            pltpu.VMEM((out_width, depth), BF16),
            pltpu.SemaphoreType.DMA((4,)),
        ],
        compiler_params=pltpu.CompilerParams(vmem_limit_bytes=18 * MIB),
        cost_estimate=pl.CostEstimate(flops=int(8e9), transcendentals=0, bytes_accessed=0),
        name="decoder_terms",
    )(ranks, table, x, y, *[pltpu.with_memory_space_constraint(a, pltpu.HBM) for a in (dirs, targets, enc, dec)])
    both_e, msg_e = pl.pallas_call(
        encoder_kernel,
        out_shape=[
            shape((2 * blocks * PER[1], COLS), F32),
            shape((message_rows(((1, blocks),)), COLS), S16),
        ],
        in_specs=[SM, SM] + [VM] * 5,
        out_specs=[VM] * 2,
        scratch_shapes=[
            pltpu.VMEM((ROWS, hidden), BF16),
            pltpu.VMEM((in_width, depth), BF16),
        ],
        compiler_params=pltpu.CompilerParams(vmem_limit_bytes=10 * MIB),
        cost_estimate=pl.CostEstimate(flops=int(6e9), transcendentals=0, bytes_accessed=0),
        name="encoder_terms",
    )(ranks, table, jac, along, cols, hid, dec_v)
    return both, msg, both_e, msg_e


def z_partner(shift):
    return lambda z: (z + shift) % 8 if z % 2 == 0 else (z - shift) % 8


Z_SHIFTS = (1, -1, 3)


def z_place(z, zb):
    place = jnp.zeros_like(zb)
    for code in range(8):
        at, odd = z, z & 1
        for bit, shift in zip((4, 2, 1), Z_SHIFTS):
            if code & bit:
                at, odd = (at + jnp.where(odd == 0, shift, -shift)) & 7, 1 - odd
        place = place + jnp.where(at == zb, code, 0)
    return place


def place_table(z, y, core, x):
    i = jnp.arange(256, dtype=jnp.int32)
    xb, zb, yb, cb = i // 64, (i // 8) % 8, (i // 2) % 4, i % 2
    zp = z_place(z, zb)
    odd, zi = zp // 4, zp % 4
    first = cb == 0
    ea = jnp.where(first, xb ^ x, yb ^ y)
    eb = jnp.where(first, yb - y, xb - x) & 3
    ap = jnp.where(ea == 0, 0, jnp.where(ea == 2, 3, jnp.where((ea == 3) == (odd == 0), 1, 2)))
    group = jnp.where(cb == core, 0, 128)
    return group + odd * 64 + ap * 16 + eb * 4 + zi


def send(value, fn):
    pairs = []
    for z in range(8):
        for y in range(4):
            for c in range(2):
                for x in range(4):
                    z2, y2, c2, x2 = fn(z, y, c, x)
                    pairs.append((((z * 4 + y) * 2 + c) * 4 + x, ((z2 * 4 + y2) * 2 + c2) * 4 + x2))
    return lax.ppermute(value, ("dp", "mp"), pairs)


def other_core(z, y, c, x):
    return (z, y, 1 - c, x)


def first_axis(flip):
    return lambda z, y, c, x: (z, y, c, x ^ flip) if c == 0 else (z, y ^ flip, c, x)


def second_axis(k):
    return lambda z, y, c, x: (z, (y + k) % 4, c, x) if c == 0 else (z, y, c, (x + k) % 4)


def z_axis(shift):
    partner = z_partner(shift)
    return lambda z, y, c, x: (partner(z), y, c, x)


def per_device(sample_inputs, sample_outputs, directions, targets, ranks, enc, dec):
    population = sample_inputs.shape[0] * lax.axis_size("dp") * lax.axis_size("mp")
    factor = 2.0 / math.sqrt(population)
    dp = lax.axis_index("dp")
    x = lax.axis_index("mp")
    z, y, core = dp // 8, (dp // 2) % 4, dp % 2
    table = place_table(z, y, core, x)
    both_d, msg_d, both_e, msg_e = own_terms(
        factor, ranks, table, sample_inputs, sample_outputs, directions, targets, enc, dec
    )
    states, waiting = [], []
    for part, both, msg in ((0, both_d, msg_d), (1, both_e, msg_e)):
        tag = "de"[part]
        arrived = [send(msg, other_core)]
        state, msgs = reduce_step(
            "core_" + tag, (part,), core_groups(part), 64,
            (((part, 128),),), (((part, 32),),) * 2, (both,), arrived,
        )
        arrived = [send(m, first_axis(f)) for m, f in zip(msgs, (1, 3))]
        state, msgs = reduce_step(
            "first_" + tag, (part,), first_groups(part), 32,
            (((part, 32),),) * 2, (((part, 16),),) * 2, state, arrived,
        )
        states += state
        waiting += [send(m, first_axis(f)) for m, f in zip(msgs, (3, 1))]
    parts = (0, 1)
    states, msgs = reduce_step(
        "join", parts, join_groups(), 8,
        (((0, 16),),) * 2 + (((1, 16),),) * 2, (sections(8),) * 3, states, waiting,
    )
    arrived = [send(m, second_axis(k)) for m, k in zip(msgs, (1, 2, 3))]
    states, msgs = reduce_step(
        "second", parts, second_groups(), 4, (sections(8),) * 3, (sections(4),), states, arrived
    )
    arrived = [send(msgs[0], z_axis(Z_SHIFTS[0]))]
    states, msgs = reduce_step(
        "z_half", parts, half_groups(2), 2, (sections(4),), (sections(2),), states, arrived
    )
    arrived = [send(msgs[0], z_axis(Z_SHIFTS[1]))]
    states, msgs = reduce_step(
        "z_quarter", parts, half_groups(1), 1, (sections(2),), (sections(1),), states, arrived
    )
    arrived = [send(msgs[0], z_axis(Z_SHIFTS[2]))]
    states, _ = reduce_step(
        "z_last", parts, last_groups(), 1, (sections(1),), (), states, arrived
    )
    return states[1], states[0]


def solution(mesh):
    both = ("dp", "mp")
    in_specs = (
        P(both, None),
        P(both, None),
        P(both, None, None),
        P(both, None, None),
        P(both),
        P(),
        P(),
    )
    return jax.shard_map(
        per_device,
        mesh=mesh,
        in_specs=in_specs,
        out_specs=(P("dp", "mp"), P("dp", "mp")),
        check_vma=False,
    )
```

time: 321 us -> 73.3 us (0.23)
  waiting for transfers between devices: 164 us -> 26.9 us
  matrix products: 69.9 us -> 0 us
  local copies, waits for them, and re-layouts: 44.4 us -> 2.02 us
  starting transfers between devices: 0.04 us -> 25.6 us
  Pallas kernels: 0 us -> 17.6 us
  other arithmetic: 16.2 us -> 0.03 us
  between operations: 14.7 us -> 0.8 us
  blocking collectives: 10.3 us -> 0 us
    reduce_scatter x1 -> x0, waiting for transfers between devices: 164 us -> none  [sum_together(): lax.psum_scatter(lines, axis, tiled=True).reshape(-1)]
    dot_general x11 -> x0, matrix products: 69.9 us -> none  [the longest x1 17.4 us: block_terms(): jnp.dot(jac_grad, decoder_weight, preferred_element_type=jnp.float32)]
    ppermute x0 -> x16, waiting for transfers between devices: none -> 26.9 us  [send(): return lax.ppermute(value, ('dp', 'mp'), pairs)]
    ppermute x0 -> x16, starting transfers between devices: none -> 25.6 us  [send(): return lax.ppermute(value, ('dp', 'mp'), pairs)]
    pallas_call x0 -> x11, Pallas kernels: none -> 17.6 us  [the longest x1 8.46 us: own_terms(): pl.pallas_call(functools.partial(decoder_kernel, factor), out_shape=[shap...]
    another operation x2 -> x0, local copies, waits for them, and re-layouts: 14.3 us -> none  [sum_together(): lines = jnp.concatenate([b.reshape(devices, -1) for b in pieces], axis=1)]
    reshape x1 -> x0, local copies, waits for them, and re-layouts: 11.8 us -> none  [sum_together(): jnp.pad(lines, ((0, 0), (0, width * 128 - lines.shape[1]))).reshape(-1, 128)]
    all_to_all x1 -> x0, blocking collectives: 10.3 us -> none  [sent_and_summed(): lax.all_to_all(pieces, axis, split_axis=0, concat_axis=0, tiled=True)]
  transfers between devices with their start and end apart: 1 -> 16, of which waited for: 1 -> 11; matrix products, arithmetic and copies ran while one was open for 0% -> 0% of each run, Pallas kernels for 0% -> 10%
where the time goes in v2:
time: 73.3 us; the launch traced here: 72.9 us
  waiting for transfers between devices  26.9 us (37%)
  starting transfers between devices  25.6 us (35%)
  Pallas kernels  17.6 us (24%)
  local copies, waits for them, and re-layouts  2.02 us (3%)
  between operations  0.8 us (1%)
    ppermute x16, waiting for transfers between devices, send(): return lax.ppermute(value, ('dp', 'mp'), pairs)  26.9 us
    ppermute x16, starting transfers between devices, send(): return lax.ppermute(value, ('dp', 'mp'), pairs)  25.6 us
    pallas_call x1, Pallas kernels, own_terms(): pl.pallas_call(functools.partial(decoder_kernel, factor), out_shape=[shap...  8.46 us
    pallas_call x1, Pallas kernels, own_terms(): pl.pallas_call(encoder_kernel, out_shape=[shape((2 * blocks * PER[1], COL...  4.6 us
    pallas_call x9, Pallas kernels, reduce_step(): pl.pallas_call(functools.partial(step_kernel, parts, groups, ins, outs),...  4.49 us
    unnamed x8, local copies, waits for them, and re-layouts  2.02 us
  transfers between devices with their start and end apart: 16, of which 11 were waited for; matrix products, arithmetic and copies ran while one was open for 0% of the time, Pallas kernels for 10%

profile of v2, /device:TPU:8, one launch (start us, length us, event | category | flops | bytes accessed | tf_op | source)
XLA Modules:
  0.0 72.9 jit_solution(11410830833920362936)
XLA Ops:
  0.7 0.0 copy-start
  0.7 0.7 copy-done
  1.4 0.0 copy-start.1
  1.4 0.7 copy-done.1
  2.1 0.0 copy-start.2
  2.1 0.7 copy-done.2
  2.8 0.0 copy-start.3
  2.8 8.5 %decoder_terms.1 = (f32[4096,512]{1,0:T(8,128)S(1)}, s16[2064,512]{1,0:T(8,128)(2,1)S(1)}, bf16[784,1024]{1,0:T(8,128)(2,1)S(1)}, f32[528,2048]{1,0:T(8,128)S(1)...) custom-call(s32[2]{0:T(128)S(1)} %copy-done.2, s32[256]{0:T(256)S(1)} %fusion.3.table, ...), custom_call_target="tpu_custom_call" | custom-call | flops 8000000000 | tf_op jit(solution)/shard_map/decoder_terms/pallas_call | solution.py:409
  11.2 0.1 collective-permute-start
  11.3 0.0 copy-done.3
  11.3 4.6 %encoder_terms.1 = (f32[2048,512]{1,0:T(8,128)S(1)}, s16[1040,512]{1,0:T(8,128)(2,1)S(1)}) custom-call(s32[2]{0:T(128)S(1)} %copy-done.3, s32[256]{0:T(256)S(1)} %fusion.3.table, bf16[784,1024]{1,0:T(8,128)(2,1)S(1)} %get-tuple-element.45.jac, f32[528,2048]{1,0:T(8,128)S(1)} %get-tuple-element.46.along, bf16[784,512]{1,0:T(8,128)(2,1)S(1)} %get-tuple-element.47.cols, ...), custom_call_target="tpu_custom_call" | custom-call | flops 6000000000 | tf_op jit(solution)/shard_map/encoder_terms/pallas_call | solution.py:435
  15.9 0.6 collective-permute-start.3
  16.5 0.0 collective-permute-done.refs_1_
  16.5 1.3 %core_d.1 = (f32[1024,512]{1,0:T(8,128)S(1)}, s16[528,512]{1,0:T(8,128)(2,1)S(1)}, s16[528,512]{1,0:T(8,128)(2,1)S(1)}) custom-call(f32[4096,512]{1,0:T(8,128)S(1)} %get-tuple-element.39.refs_0_, s16[2064,512]{1,0:T(8,128)(2,1)S(1)} %collective-permute-done.refs_1_), custom_call_target="tpu_custom_call" | custom-call | flops 12800000000 | tf_op jit(solution)/shard_map/core_d/pallas_call | solution.py:168
  17.8 1.6 %collective-permute-start.1 = (s16[528,512]{1,0:T(8,128)(2,1)S(1)}, s16[528,512]{1,0:T(8,128)(2,1)S(1)}, u32[]{:S(2)}, u32[]{:S(2)}) collective-permute-start(s16[528,512]{1,0:T(8,128)(2,1)S(1)} %get-tuple-element.42), channel_id=1, source_target_pairs={{0,1},{1,0},{2,3},{3,2},{4,12},{5,13},{6,14},{7,15},{8,9},{9,8},{1... | collective-permute-start | bytes 1622024 | tf_op jit(solution)/shard_map/ppermute | solution.py:493
  19.4 2.1 %collective-permute-start.2 = (s16[528,512]{1,0:T(8,128)(2,1)S(1)}, s16[528,512]{1,0:T(8,128)(2,1)S(1)}, u32[]{:S(2)}, u32[]{:S(2)}) collective-permute-start(s16[528,512]{1,0:T(8,128)(2,1)S(1)} %get-tuple-element.43), channel_id=1, source_target_pairs={{0,3},{1,2},{2,1},{3,0},{4,28},{5,29},{6,30},{7,31},{8,11},{9,10},... | collective-permute-start | bytes 1622024 | tf_op jit(solution)/shard_map/ppermute | solution.py:493
  21.5 0.0 collective-permute-done.3.refs_1_
  21.5 0.7 core_e.1
  22.2 0.9 %collective-permute-start.4 = (s16[272,512]{1,0:T(8,128)(2,1)S(1)}, s16[272,512]{1,0:T(8,128)(2,1)S(1)}, u32[]{:S(2)}, u32[]{:S(2)}) collective-permute-start(s16[272,512]{1,0:T(8,128)(2,1)S(1)} %get-tuple-element.53), channel_id=1, source_target_pairs={{0,1},{1,0},{2,3},{3,2},{4,12},{5,13},{6,14},{7,15},{8,9},{9,8},{1... | collective-permute-start | bytes 835592 | tf_op jit(solution)/shard_map/ppermute | solution.py:493
  23.0 0.6 collective-permute-start.5
  23.7 3.6 %collective-permute-done.1.refs_1_ = s16[528,512]{1,0:T(8,128)(2,1)S(1)} collective-permute-done((s16[528,512]{1,0:T(8,128)(2,1)S(1)}, s16[528,512]{1,0:T(8,128)(2,1)S(1)}, u32[]{:S(2)}, u32[]{:S(2)}) %collective-permute-start.1) | collective-permute-done | bytes 540704 | tf_op jit(solution)/shard_map/ppermute | solution.py:493
  27.3 2.7 %collective-permute-done.2.refs_2_ = s16[528,512]{1,0:T(8,128)(2,1)S(1)} collective-permute-done((s16[528,512]{1,0:T(8,128)(2,1)S(1)}, s16[528,512]{1,0:T(8,128)(2,1)S(1)}, u32[]{:S(2)}, u32[]{:S(2)}) %collective-permute-start.2) | collective-permute-done | bytes 540704 | tf_op jit(solution)/shard_map/ppermute | solution.py:493
  30.0 0.7 first_d.1
  30.7 2.2 %collective-permute-start.6 = (s16[272,512]{1,0:T(8,128)(2,1)S(1)}, s16[272,512]{1,0:T(8,128)(2,1)S(1)}, u32[]{:S(2)}, u32[]{:S(2)}) collective-permute-start(s16[272,512]{1,0:T(8,128)(2,1)S(1)} %get-tuple-element.56), channel_id=1, source_target_pairs={{0,3},{1,2},{2,1},{3,0},{4,28},{5,29},{6,30},{7,31},{8,11},{9,10},... | collective-permute-start | bytes 835592 | tf_op jit(solution)/shard_map/ppermute | solution.py:493
  32.8 0.0 collective-permute-start.7
  32.8 0.0 collective-permute-done.4.refs_1_
  32.8 0.1 collective-permute-done.5.refs_2_
  32.9 0.4 first_e.1
  33.3 2.2 %collective-permute-start.8 = (s16[144,512]{1,0:T(8,128)(2,1)S(1)}, s16[144,512]{1,0:T(8,128)(2,1)S(1)}, u32[]{:S(2)}, u32[]{:S(2)}) collective-permute-start(s16[144,512]{1,0:T(8,128)(2,1)S(1)} %get-tuple-element.58), channel_id=1, source_target_pairs={{0,3},{1,2},{2,1},{3,0},{4,28},{5,29},{6,30},{7,31},{8,11},{9,10},... | collective-permute-start | bytes 442376 | tf_op jit(solution)/shard_map/ppermute | solution.py:493
  35.5 0.4 collective-permute-start.9
  35.9 4.2 %collective-permute-done.8.refs_4_ = s16[144,512]{1,0:T(8,128)(2,1)S(1)} collective-permute-done((s16[144,512]{1,0:T(8,128)(2,1)S(1)}, s16[144,512]{1,0:T(8,128)(2,1)S(1)}, u32[]{:S(2)}, u32[]{:S(2)}) %collective-permute-start.8) | collective-permute-done | bytes 147488 | tf_op jit(solution)/shard_map/ppermute | solution.py:493
  40.1 0.9 %collective-permute-done.9.refs_5_ = s16[144,512]{1,0:T(8,128)(2,1)S(1)} collective-permute-done((s16[144,512]{1,0:T(8,128)(2,1)S(1)}, s16[144,512]{1,0:T(8,128)(2,1)S(1)}, u32[]{:S(2)}, u32[]{:S(2)}) %collective-permute-start.9) | collective-permute-done | bytes 147488 | tf_op jit(solution)/shard_map/ppermute | solution.py:493
  41.0 0.0 collective-permute-done.6.refs_2_
  41.0 0.0 collective-permute-done.7.refs_3_
  41.0 0.5 join.1
  41.5 2.3 %collective-permute-start.10 = (s16[208,512]{1,0:T(8,128)(2,1)S(1)}, s16[208,512]{1,0:T(8,128)(2,1)S(1)}, u32[]{:S(2)}, u32[]{:S(2)}) collective-permute-start(s16[208,512]{1,0:T(8,128)(2,1)S(1)} %get-tuple-element.62), channel_id=1, source_target_pairs={{0,8},{1,9},{2,10},{3,11},{4,5},{5,6},{6,7},{7,4},{8,16},{9,17},{1... | collective-permute-start | bytes 638984 | tf_op jit(solution)/shard_map/ppermute | solution.py:493
  43.8 0.3 collective-permute-start.11
  44.1 2.4 %collective-permute-start.12 = (s16[208,512]{1,0:T(8,128)(2,1)S(1)}, s16[208,512]{1,0:T(8,128)(2,1)S(1)}, u32[]{:S(2)}, u32[]{:S(2)}) collective-permute-start(s16[208,512]{1,0:T(8,128)(2,1)S(1)} %get-tuple-element.64), channel_id=1, source_target_pairs={{0,24},{1,25},{2,26},{3,27},{4,7},{5,4},{6,5},{7,6},{8,0},{9,1},{1... | collective-permute-start | bytes 638984 | tf_op jit(solution)/shard_map/ppermute | solution.py:493
  46.5 0.9 %collective-permute-done.10.refs_2_ = s16[208,512]{1,0:T(8,128)(2,1)S(1)} collective-permute-done((s16[208,512]{1,0:T(8,128)(2,1)S(1)}, s16[208,512]{1,0:T(8,128)(2,1)S(1)}, u32[]{:S(2)}, u32[]{:S(2)}) %collective-permute-start.10) | collective-permute-done | bytes 213024 | tf_op jit(solution)/shard_map/ppermute | solution.py:493
  47.4 3.8 %collective-permute-done.11.refs_3_ = s16[208,512]{1,0:T(8,128)(2,1)S(1)} collective-permute-done((s16[208,512]{1,0:T(8,128)(2,1)S(1)}, s16[208,512]{1,0:T(8,128)(2,1)S(1)}, u32[]{:S(2)}, u32[]{:S(2)}) %collective-permute-start.11) | collective-permute-done | bytes 213024 | tf_op jit(solution)/shard_map/ppermute | solution.py:493
  51.2 1.0 %collective-permute-done.12.refs_4_ = s16[208,512]{1,0:T(8,128)(2,1)S(1)} collective-permute-done((s16[208,512]{1,0:T(8,128)(2,1)S(1)}, s16[208,512]{1,0:T(8,128)(2,1)S(1)}, u32[]{:S(2)}, u32[]{:S(2)}) %collective-permute-start.12) | collective-permute-done | bytes 213024 | tf_op jit(solution)/shard_map/ppermute | solution.py:493
  52.2 0.2 second.1
  52.4 2.0 %collective-permute-start.13 = (s16[112,512]{1,0:T(8,128)(2,1)S(1)}, s16[112,512]{1,0:T(8,128)(2,1)S(1)}, u32[]{:S(2)}, u32[]{:S(2)}) collective-permute-start(s16[112,512]{1,0:T(8,128)(2,1)S(1)} %get-tuple-element.67), channel_id=1, source_target_pairs={{0,32},{1,33},{2,34},{3,35},{4,36},{5,37},{6,38},{7,39},{8,40},{9,... | collective-permute-start | bytes 344072 | tf_op jit(solution)/shard_map/ppermute | solution.py:493
  54.5 2.9 %collective-permute-done.13.refs_2_ = s16[112,512]{1,0:T(8,128)(2,1)S(1)} collective-permute-done((s16[112,512]{1,0:T(8,128)(2,1)S(1)}, s16[112,512]{1,0:T(8,128)(2,1)S(1)}, u32[]{:S(2)}, u32[]{:S(2)}) %collective-permute-start.13) | collective-permute-done | bytes 114720 | tf_op jit(solution)/shard_map/ppermute | solution.py:493
  57.3 0.1 z_half.1
  57.4 6.5 %collective-permute-start.14 = (s16[64,512]{1,0:T(8,128)(2,1)S(1)}, s16[64,512]{1,0:T(8,128)(2,1)S(1)}, u32[]{:S(2)}, u32[]{:S(2)}) collective-permute-start(s16[64,512]{1,0:T(8,128)(2,1)S(1)} %get-tuple-element.70), channel_id=1, source_target_pairs={{0,224},{1,225},{2,226},{3,227},{4,228},{5,229},{6,230},{7,231},{8... | collective-permute-start | bytes 196616 | tf_op jit(solution)/shard_map/ppermute | solution.py:493
  63.9 2.2 %collective-permute-done.14.refs_2_ = s16[64,512]{1,0:T(8,128)(2,1)S(1)} collective-permute-done((s16[64,512]{1,0:T(8,128)(2,1)S(1)}, s16[64,512]{1,0:T(8,128)(2,1)S(1)}, u32[]{:S(2)}, u32[]{:S(2)}) %collective-permute-start.14) | collective-permute-done | bytes 65568 | tf_op jit(solution)/shard_map/ppermute | solution.py:493
  66.1 0.1 z_quarter.1
  66.2 1.6 %collective-permute-start.15 = (s16[48,512]{1,0:T(8,128)(2,1)S(1)}, s16[48,512]{1,0:T(8,128)(2,1)S(1)}, u32[]{:S(2)}, u32[]{:S(2)}) collective-permute-start(s16[48,512]{1,0:T(8,128)(2,1)S(1)} %get-tuple-element.73), channel_id=1, source_target_pairs={{0,96},{1,97},{2,98},{3,99},{4,100},{5,101},{6,102},{7,103},{8,104... | collective-permute-start | bytes 147464 | tf_op jit(solution)/shard_map/ppermute | solution.py:493
  67.8 4.5 %collective-permute-done.15.refs_2_ = s16[48,512]{1,0:T(8,128)(2,1)S(1)} collective-permute-done((s16[48,512]{1,0:T(8,128)(2,1)S(1)}, s16[48,512]{1,0:T(8,128)(2,1)S(1)}, u32[]{:S(2)}, u32[]{:S(2)}) %collective-permute-start.15) | collective-permute-done | bytes 49184 | tf_op jit(solution)/shard_map/ppermute | solution.py:493
  72.3 0.6 z_last.1
  (1 shorter events, 0.0 us)
Async XLA Ops:
  0.7 0.7 copy-start
  1.4 0.7 copy-start.1
  2.1 0.7 copy-start.2
  2.8 8.6 %copy-start.3 = (s32[2]{0:T(128)S(1)}, s32[2]{0:T(128)}, u32[]{:S(2)}) copy-start(s32[2]{0:T(128)} %ranks.3) | copy-start | bytes 28
  11.2 5.3 %collective-permute-start = (s16[2064,512]{1,0:T(8,128)(2,1)S(1)}, s16[2064,512]{1,0:T(8,128)(2,1)S(1)}, u32[]{:S(2)}, u32[]{:S(2)}) collective-permute-start(s16[2064,512]{1,0:T(8,128)(2,1)S(1)} %get-tuple-element.40), channel_id=1, source_target_pairs={{0,4},{1,5},{2,6},{3,7},{4,0},{5,1},{6,2},{7,3},{8,12},{9,13},{10,... | collective-permute-start | bytes 6340616 | tf_op jit(solution)/shard_map/ppermute | solution.py:493
  15.9 5.6 %collective-permute-start.3 = (s16[1040,512]{1,0:T(8,128)(2,1)S(1)}, s16[1040,512]{1,0:T(8,128)(2,1)S(1)}, u32[]{:S(2)}, u32[]{:S(2)}) collective-permute-start(s16[1040,512]{1,0:T(8,128)(2,1)S(1)} %get-tuple-element.51), channel_id=1, source_target_pairs={{0,4},{1,5},{2,6},{3,7},{4,0},{5,1},{6,2},{7,3},{8,12},{9,13},{10,... | collective-permute-start | bytes 3194888 | tf_op jit(solution)/shard_map/ppermute | solution.py:493
  17.8 9.4 %collective-permute-start.1 = (s16[528,512]{1,0:T(8,128)(2,1)S(1)}, s16[528,512]{1,0:T(8,128)(2,1)S(1)}, u32[]{:S(2)}, u32[]{:S(2)}) collective-permute-start(s16[528,512]{1,0:T(8,128)(2,1)S(1)} %get-tuple-element.42), channel_id=1, source_target_pairs={{0,1},{1,0},{2,3},{3,2},{4,12},{5,13},{6,14},{7,15},{8,9},{9,8},{1... | collective-permute-start | bytes 1622024 | tf_op jit(solution)/shard_map/ppermute | solution.py:493
  19.4 10.6 %collective-permute-start.2 = (s16[528,512]{1,0:T(8,128)(2,1)S(1)}, s16[528,512]{1,0:T(8,128)(2,1)S(1)}, u32[]{:S(2)}, u32[]{:S(2)}) collective-permute-start(s16[528,512]{1,0:T(8,128)(2,1)S(1)} %get-tuple-element.43), channel_id=1, source_target_pairs={{0,3},{1,2},{2,1},{3,0},{4,28},{5,29},{6,30},{7,31},{8,11},{9,10},... | collective-permute-start | bytes 1622024 | tf_op jit(solution)/shard_map/ppermute | solution.py:493
  22.2 10.7 %collective-permute-start.4 = (s16[272,512]{1,0:T(8,128)(2,1)S(1)}, s16[272,512]{1,0:T(8,128)(2,1)S(1)}, u32[]{:S(2)}, u32[]{:S(2)}) collective-permute-start(s16[272,512]{1,0:T(8,128)(2,1)S(1)} %get-tuple-element.53), channel_id=1, source_target_pairs={{0,1},{1,0},{2,3},{3,2},{4,12},{5,13},{6,14},{7,15},{8,9},{9,8},{1... | collective-permute-start | bytes 835592 | tf_op jit(solution)/shard_map/ppermute | solution.py:493
  23.0 9.9 %collective-permute-start.5 = (s16[272,512]{1,0:T(8,128)(2,1)S(1)}, s16[272,512]{1,0:T(8,128)(2,1)S(1)}, u32[]{:S(2)}, u32[]{:S(2)}) collective-permute-start(s16[272,512]{1,0:T(8,128)(2,1)S(1)} %get-tuple-element.54), channel_id=1, source_target_pairs={{0,3},{1,2},{2,1},{3,0},{4,28},{5,29},{6,30},{7,31},{8,11},{9,10},... | collective-permute-start | bytes 835592 | tf_op jit(solution)/shard_map/ppermute | solution.py:493
  30.7 10.3 %collective-permute-start.6 = (s16[272,512]{1,0:T(8,128)(2,1)S(1)}, s16[272,512]{1,0:T(8,128)(2,1)S(1)}, u32[]{:S(2)}, u32[]{:S(2)}) collective-permute-start(s16[272,512]{1,0:T(8,128)(2,1)S(1)} %get-tuple-element.56), channel_id=1, source_target_pairs={{0,3},{1,2},{2,1},{3,0},{4,28},{5,29},{6,30},{7,31},{8,11},{9,10},... | collective-permute-start | bytes 835592 | tf_op jit(solution)/shard_map/ppermute | solution.py:493
  32.8 8.1 %collective-permute-start.7 = (s16[272,512]{1,0:T(8,128)(2,1)S(1)}, s16[272,512]{1,0:T(8,128)(2,1)S(1)}, u32[]{:S(2)}, u32[]{:S(2)}) collective-permute-start(s16[272,512]{1,0:T(8,128)(2,1)S(1)} %get-tuple-element.57), channel_id=1, source_target_pairs={{0,1},{1,0},{2,3},{3,2},{4,12},{5,13},{6,14},{7,15},{8,9},{9,8},{1... | collective-permute-start | bytes 835592 | tf_op jit(solution)/shard_map/ppermute | solution.py:493
  33.3 6.8 %collective-permute-start.8 = (s16[144,512]{1,0:T(8,128)(2,1)S(1)}, s16[144,512]{1,0:T(8,128)(2,1)S(1)}, u32[]{:S(2)}, u32[]{:S(2)}) collective-permute-start(s16[144,512]{1,0:T(8,128)(2,1)S(1)} %get-tuple-element.58), channel_id=1, source_target_pairs={{0,3},{1,2},{2,1},{3,0},{4,28},{5,29},{6,30},{7,31},{8,11},{9,10},... | collective-permute-start | bytes 442376 | tf_op jit(solution)/shard_map/ppermute | solution.py:493
  35.5 5.5 %collective-permute-start.9 = (s16[144,512]{1,0:T(8,128)(2,1)S(1)}, s16[144,512]{1,0:T(8,128)(2,1)S(1)}, u32[]{:S(2)}, u32[]{:S(2)}) collective-permute-start(s16[144,512]{1,0:T(8,128)(2,1)S(1)} %get-tuple-element.59), channel_id=1, source_target_pairs={{0,1},{1,0},{2,3},{3,2},{4,12},{5,13},{6,14},{7,15},{8,9},{9,8},{1... | collective-permute-start | bytes 442376 | tf_op jit(solution)/shard_map/ppermute | solution.py:493
  41.5 5.9 %collective-permute-start.10 = (s16[208,512]{1,0:T(8,128)(2,1)S(1)}, s16[208,512]{1,0:T(8,128)(2,1)S(1)}, u32[]{:S(2)}, u32[]{:S(2)}) collective-permute-start(s16[208,512]{1,0:T(8,128)(2,1)S(1)} %get-tuple-element.62), channel_id=1, source_target_pairs={{0,8},{1,9},{2,10},{3,11},{4,5},{5,6},{6,7},{7,4},{8,16},{9,17},{1... | collective-permute-start | bytes 638984 | tf_op jit(solution)/shard_map/ppermute | solution.py:493
  43.8 7.5 %collective-permute-start.11 = (s16[208,512]{1,0:T(8,128)(2,1)S(1)}, s16[208,512]{1,0:T(8,128)(2,1)S(1)}, u32[]{:S(2)}, u32[]{:S(2)}) collective-permute-start(s16[208,512]{1,0:T(8,128)(2,1)S(1)} %get-tuple-element.63), channel_id=1, source_target_pairs={{0,16},{1,17},{2,18},{3,19},{4,6},{5,7},{6,4},{7,5},{8,24},{9,25},... | collective-permute-start | bytes 638984 | tf_op jit(solution)/shard_map/ppermute | solution.py:493
  44.1 8.1 %collective-permute-start.12 = (s16[208,512]{1,0:T(8,128)(2,1)S(1)}, s16[208,512]{1,0:T(8,128)(2,1)S(1)}, u32[]{:S(2)}, u32[]{:S(2)}) collective-permute-start(s16[208,512]{1,0:T(8,128)(2,1)S(1)} %get-tuple-element.64), channel_id=1, source_target_pairs={{0,24},{1,25},{2,26},{3,27},{4,7},{5,4},{6,5},{7,6},{8,0},{9,1},{1... | collective-permute-start | bytes 638984 | tf_op jit(solution)/shard_map/ppermute | solution.py:493
  52.4 4.9 %collective-permute-start.13 = (s16[112,512]{1,0:T(8,128)(2,1)S(1)}, s16[112,512]{1,0:T(8,128)(2,1)S(1)}, u32[]{:S(2)}, u32[]{:S(2)}) collective-permute-start(s16[112,512]{1,0:T(8,128)(2,1)S(1)} %get-tuple-element.67), channel_id=1, source_target_pairs={{0,32},{1,33},{2,34},{3,35},{4,36},{5,37},{6,38},{7,39},{8,40},{9,... | collective-permute-start | bytes 344072 | tf_op jit(solution)/shard_map/ppermute | solution.py:493
  57.4 8.7 %collective-permute-start.14 = (s16[64,512]{1,0:T(8,128)(2,1)S(1)}, s16[64,512]{1,0:T(8,128)(2,1)S(1)}, u32[]{:S(2)}, u32[]{:S(2)}) collective-permute-start(s16[64,512]{1,0:T(8,128)(2,1)S(1)} %get-tuple-element.70), channel_id=1, source_target_pairs={{0,224},{1,225},{2,226},{3,227},{4,228},{5,229},{6,230},{7,231},{8... | collective-permute-start | bytes 196616 | tf_op jit(solution)/shard_map/ppermute | solution.py:493
  66.2 6.1 %collective-permute-start.15 = (s16[48,512]{1,0:T(8,128)(2,1)S(1)}, s16[48,512]{1,0:T(8,128)(2,1)S(1)}, u32[]{:S(2)}, u32[]{:S(2)}) collective-permute-start(s16[48,512]{1,0:T(8,128)(2,1)S(1)} %get-tuple-element.73), channel_id=1, source_target_pairs={{0,96},{1,97},{2,98},{3,99},{4,100},{5,101},{6,102},{7,103},{8,104... | collective-permute-start | bytes 147464 | tf_op jit(solution)/shard_map/ppermute | solution.py:493
